TPU v7x, 256 devices: a whole 4x4x8 slice. The times are simulated.
256 devices in a mesh: unit: 4 (over x), replica: 16 (over z, core), model: 4 (over y).
Axes of the slice: x: 4, y: 4, z: 8, core: 2. Of those that a mesh axis runs over, the one named last changes fastest.
Arguments:
- slope_up: float32 [64, 768, 3072], P(('unit', 'replica'), None, 'model'), parts along dimension 0, may hold values from -0.875 to 0.875
- slope_down: float32 [64, 3072, 768], P(('unit', 'replica'), 'model'), parts along dimension 0, may hold values from -0.875 to 0.875
- slope_query: float32 [64, 768, 768], P(('unit', 'replica'), None, 'model'), parts along dimension 0, may hold values from -0.875 to 0.875
- slope_key: float32 [64, 768, 768], P(('unit', 'replica'), None, 'model'), parts along dimension 0, may hold values from -0.875 to 0.875
- slope_value: float32 [64, 768, 768], P(('unit', 'replica'), None, 'model'), parts along dimension 0, may hold values from -0.875 to 0.875
- slope_mixed: float32 [64, 768, 768], P(('unit', 'replica'), 'model'), parts along dimension 0, may hold values from -0.875 to 0.875
- slope_norm: float32 [64, 768], P(('unit', 'replica')), parts along dimension 0, may hold values from -8 to 8
- param_up: float32 [3072, 3072], P(('unit', 'replica'), 'model'), parts along dimension 0, may hold values from -0.21875 to 0.21875
- param_down: float32 [12288, 768], P(('unit', 'model'), 'replica'), parts along dimension 0, may hold values from -0.109375 to 0.109375
- param_query: float32 [3072, 768], P(('unit', 'replica'), 'model'), parts along dimension 0, may hold values from -0.21875 to 0.21875
- param_key: float32 [3072, 768], P(('unit', 'replica'), 'model'), parts along dimension 0, may hold values from -0.21875 to 0.21875
- param_value: float32 [3072, 768], P(('unit', 'replica'), 'model'), parts along dimension 0, may hold values from -0.21875 to 0.21875
- param_mixed: float32 [3072, 768], P(('unit', 'model'), 'replica'), parts along dimension 0, may hold values from -0.21875 to 0.21875
- param_norm: float32 [3072], P(('unit', 'replica')), parts along dimension 0, may hold values from 0.25 to 1.75
Outputs:
- half_up: bfloat16 [3072, 3072], P('unit', 'model'), parts along dimension 0
- half_down: bfloat16 [12288, 768], P(('unit', 'model')), parts along dimension 0
- half_query: bfloat16 [3072, 768], P('unit', 'model'), parts along dimension 0
- half_key: bfloat16 [3072, 768], P('unit', 'model'), parts along dimension 0
- half_value: bfloat16 [3072, 768], P('unit', 'model'), parts along dimension 0
- half_mixed: bfloat16 [3072, 768], P(('unit', 'model')), parts along dimension 0
- half_norm: bfloat16 [3072], P('unit'), parts along dimension 0
- next_up: float32 [3072, 3072], P(('unit', 'replica'), 'model'), parts along dimension 0
- next_down: float32 [12288, 768], P(('unit', 'model'), 'replica'), parts along dimension 0
- next_query: float32 [3072, 768], P(('unit', 'replica'), 'model'), parts along dimension 0
- next_key: float32 [3072, 768], P(('unit', 'replica'), 'model'), parts along dimension 0
- next_value: float32 [3072, 768], P(('unit', 'replica'), 'model'), parts along dimension 0
- next_mixed: float32 [3072, 768], P(('unit', 'model'), 'replica'), parts along dimension 0
- next_norm: float32 [3072], P(('unit', 'replica')), parts along dimension 0
There are 4 independent parts, one for each index of `unit`. A program takes and returns all parts, laid end to end along the dimension named above; each array names one. Nothing has to cross between parts.
All inputs are finite; a program needn't handle non-finite values.
Results may differ from a plain program's by a relative error of at most 0.001.
Values may be sent and summed in bfloat16 or wider, within the bound.
No kernel may reach another device: no remote copies, remote signals or barrier semaphores. Data moves between devices by JAX's collectives and lax.ppermute only.
A program may use at most 64 MiB of HBM per device.

v0:
```python
import jax
import jax.numpy as jnp
from jax import lax
from jax.sharding import PartitionSpec as P

learn_rate = 0.3


def split_up(array, dim, size):
    lengths = array.shape
    parts = array.reshape(*lengths[:dim], size, lengths[dim] // size, *lengths[dim + 1 :])
    return jnp.moveaxis(parts, dim, 0)


def sum_together(arrays, axis, dims):
    size = lax.axis_size(axis)
    parts = [split_up(a, dim, size) for a, dim in zip(arrays, dims)]
    lines = jnp.concatenate([b.reshape(size, -1) for b in parts], axis=1)
    width = max(16, -(-lines.shape[1] // 1024) * 8)
    lines = jnp.pad(lines, ((0, 0), (0, width * 128 - lines.shape[1]))).reshape(-1, 128)
    vector, at, finished = (lax.psum_scatter(lines, axis, tiled=True).reshape(-1), 0, [])
    for b in parts:
        part = b[0]
        finished.append(vector[at : at + part.size].reshape(part.shape))
        at += part.size
    return tuple(finished)


def rows_first(arrays, axis, dims):
    turned = [jnp.moveaxis(a, dim, 0) for a, dim in zip(arrays, dims)]
    both = jnp.concatenate([t.reshape(len(t), -1) for t in turned], axis=1)
    out, at, finished = (lax.all_gather(both, axis, axis=0, tiled=True), 0, [])
    for t, dim in zip(turned, dims):
        slab = out[:, at : at + t[0].size].reshape(-1, *t.shape[1:])
        finished.append(jnp.moveaxis(slab, 0, dim))
        at += t[0].size
    return tuple(finished)


def shards(
    slope_up,
    slope_down,
    slope_query,
    slope_key,
    slope_value,
    slope_mixed,
    slope_norm,
    param_up,
    param_down,
    param_query,
    param_key,
    param_value,
    param_mixed,
    param_norm,
):
    mean_up, mean_down, mean_query, mean_key, mean_value, mean_mixed, mean_norm = sum_together(
        (
            slope_up[0],
            slope_down[0],
            slope_query[0],
            slope_key[0],
            slope_value[0],
            slope_mixed[0],
            slope_norm[0],
        ),
        "replica",
        (0, 1, 0, 0, 0, 1, 0),
    )
    mean_rate = lax.axis_size("replica") ** (-0.5)
    mean_up = mean_up * mean_rate
    mean_down = mean_down * mean_rate
    mean_query = mean_query * mean_rate
    mean_key = mean_key * mean_rate
    mean_value = mean_value * mean_rate
    mean_mixed = mean_mixed * mean_rate
    mean_norm = mean_norm * mean_rate
    next_up = param_up - learn_rate * mean_up
    next_down = param_down - learn_rate * mean_down
    next_query = param_query - learn_rate * mean_query
    next_key = param_key - learn_rate * mean_key
    next_value = param_value - learn_rate * mean_value
    next_mixed = param_mixed - learn_rate * mean_mixed
    next_norm = param_norm - learn_rate * mean_norm
    half_up, half_down, half_query, half_key, half_value, half_mixed, half_norm = rows_first(
        (
            next_up.astype(jnp.bfloat16),
            next_down.astype(jnp.bfloat16),
            next_query.astype(jnp.bfloat16),
            next_key.astype(jnp.bfloat16),
            next_value.astype(jnp.bfloat16),
            next_mixed.astype(jnp.bfloat16),
            next_norm.astype(jnp.bfloat16),
        ),
        "replica",
        (0, 1, 0, 0, 0, 1, 0),
    )
    return (
        half_up,
        half_down,
        half_query,
        half_key,
        half_value,
        half_mixed,
        half_norm,
        next_up,
        next_down,
        next_query,
        next_key,
        next_value,
        next_mixed,
        next_norm,
    )


def solution(mesh):
    placed = (
        P(("unit", "replica"), None, "model"),
        P(("unit", "replica"), "model", None),
        P(("unit", "replica"), None, "model"),
        P(("unit", "replica"), None, "model"),
        P(("unit", "replica"), None, "model"),
        P(("unit", "replica"), "model", None),
        P(("unit", "replica"), None),
        P(("unit", "replica"), "model"),
        P(("unit", "model"), "replica"),
        P(("unit", "replica"), "model"),
        P(("unit", "replica"), "model"),
        P(("unit", "replica"), "model"),
        P(("unit", "model"), "replica"),
        P(("unit", "replica")),
    )
    return jax.shard_map(
        shards,
        mesh=mesh,
        in_specs=placed,
        out_specs=(
            P("unit", "model"),
            P(("unit", "model"), None),
            P("unit", "model"),
            P("unit", "model"),
            P("unit", "model"),
            P(("unit", "model"), None),
            P("unit"),
            P(("unit", "replica"), "model"),
            P(("unit", "model"), "replica"),
            P(("unit", "replica"), "model"),
            P(("unit", "replica"), "model"),
            P(("unit", "replica"), "model"),
            P(("unit", "model"), "replica"),
            P(("unit", "replica")),
        ),
        check_vma=False,
    )
```

profile of v0, /device:TPU:1, one launch (start us, length us, event | category | flops | bytes accessed | tf_op | source)
XLA Modules:
  0.0 258.9 jit_solution(8501076146839965189)
XLA Ops:
  7.2 1.9 reshape_reshape_squeeze.12
  9.1 1.6 constant_dynamic-update-slice_fusion.6
  10.7 2.0 copy.69
  12.7 4.1 %copy.70 = f32[16,768,48]{2,1,0:T(8,128)} copy(f32[16,768,48]{1,2,0:T(8,128)S(1)} %bitcast.19) | data formatting | bytes 4718592 | tf_op jit(solution)/shard_map/transpose | solution.py:12
  16.8 7.3 %reshape.76 = f32[16,36864]{1,0:T(8,128)S(1)} reshape(f32[16,768,48]{2,1,0:T(8,128)} %copy.70) | data formatting | bytes 4718592 | tf_op jit(solution)/shard_map/reshape | solution.py:18
  24.1 1.3 copy.71
  25.5 1.1 reshape_reshape_squeeze.13
  26.6 1.3 copy.72
  27.9 1.1 reshape_reshape_squeeze.14
  29.0 1.3 copy.73
  30.4 1.1 reshape_reshape_squeeze.15
  31.5 1.3 copy.74
  32.8 1.7 copy.75
  34.5 3.5 %reshape.77 = f32[16,9216]{1,0:T(8,128)} reshape(f32[16,192,48]{2,1,0:T(8,128)} %copy.75) | data formatting | bytes 1179648 | tf_op jit(solution)/shard_map/reshape | solution.py:18
  38.1 1.6 constant_dynamic-update-slice_fusion.5
  39.7 0.9 constant_dynamic-update-slice_fusion.4
  41.4 0.9 constant_dynamic-update-slice_fusion.2
  42.3 0.9 constant_dynamic-update-slice_fusion.1
  43.8 6.4 %pad.4 = f32[16,111616]{1,0:T(8,128)} pad(f32[16,110640]{1,0:T(8,128)} %constant_dynamic-update-slice_fusion, f32[]{:T(128)} %constant.8.clone.1), padding=0_0x0_976 | pad | bytes 14224388 | tf_op jit(solution)/shard_map/jit(_pad)/pad | solution.py:20
  50.1 5.5 %reshape.78 = f32[13952,128]{1,0:T(8,128)} reshape(f32[16,111616]{1,0:T(8,128)} %pad.4) | data formatting | bytes 14286848 | tf_op jit(solution)/shard_map/reshape | solution.py:20
  57.5 132.0 %all-reduce.4.cloned.1.call-done = f32[13952,128]{1,0:T(8,128)} async-done(((f32[13952,128]{1,0:T(8,128)}), f32[13952,128]{1,0:T(8,128)}) %all-reduce.4.cloned.1.call-update) | async-done | bytes 7143440
  189.5 1.0 dynamic-slice_multiply_fusion
  190.9 0.9 dynamic-slice_multiply_fusion.2
  192.2 1.1 dynamic-slice_bitcast_fusion
  198.0 42.8 %all-gather.2.cloned.1.call-done = bf16[768,2305]{1,0:T(8,128)(2,1)} async-done(((bf16[48,2305]{1,0:T(8,128)(2,1)}), bf16[768,2305]{1,0:T(8,128)(2,1)}) %all-gather.2.cloned.1.call-update) | async-done | bytes 3540496 | tf_op jit(solution)/shard_map/all_gather | solution.py:32
  240.8 2.8 %slice_bitcast_fusion = (bf16[768,768]{0,1:T(8,128)(2,1)S(1)}, bf16[768,768]{1,0:T(8,128)(2,1)}) fusion(bf16[768,2305]{1,0:T(8,128)(2,1)} %all-gather.2.cloned.1.call-done), kind=kLoop, calls=%fused_computation | loop fusion | bytes 4718592 | tf_op jit(solution)/shard_map/transpose | solution.py:35
  243.6 1.4 copy.79
  245.0 1.9 slice_bitcast_fusion.1
  246.9 0.9 copy.80
  247.8 0.9 copy.81
  248.7 0.9 copy.82
  250.4 1.7 slice_reduce_fusion
  (52 shorter events, 9.1 us)
Async XLA Ops:
  7.2 182.3 %all-reduce.4.cloned.1.call-start = ((), (), s32[]{:S(2)}) async-start(), calls=%async_computation.1 | async-start | bytes 14286848
  24.1 13.9 %copy-start.10 = (f32[1,768]{1,0:T(1,128)S(1)}, f32[1,768]{1,0:T(1,128)}, u32[]{:S(2)}) copy-start(f32[1,768]{1,0:T(1,128)} %param.20) | copy-start | bytes 9220
  34.5 5.1 %copy-start = (f32[16,9216]{1,0:T(8,128)S(1)}, f32[16,9216]{1,0:T(8,128)}, u32[]{:S(2)}) copy-start(f32[16,9216]{1,0:T(8,128)} %reshape_reshape_squeeze.13) | copy-start | bytes 1769476
  34.5 6.0 %copy-start.1 = (f32[16,9216]{1,0:T(8,128)S(1)}, f32[16,9216]{1,0:T(8,128)}, u32[]{:S(2)}) copy-start(f32[16,9216]{1,0:T(8,128)} %reshape_reshape_squeeze.14) | copy-start | bytes 1769476
  38.1 3.3 %copy-start.2 = (f32[16,9216]{1,0:T(8,128)S(1)}, f32[16,9216]{1,0:T(8,128)}, u32[]{:S(2)}) copy-start(f32[16,9216]{1,0:T(8,128)} %reshape_reshape_squeeze.15) | copy-start | bytes 1769476
  38.1 4.2 %copy-start.3 = (f32[16,9216]{1,0:T(8,128)S(1)}, f32[16,9216]{1,0:T(8,128)}, u32[]{:S(2)}) copy-start(f32[16,9216]{1,0:T(8,128)} %reshape.77) | copy-start | bytes 1769476
  55.6 0.7 copy-start.12
  55.6 137.6 %copy-start.11 = (f32[48]{0:T(128)S(1)}, f32[48]{0:T(128)}, u32[]{:S(2)}) copy-start(f32[48]{0:T(128)} %param.27) | copy-start | bytes 580
  55.6 138.3 %copy-start.4 = (f32[48,768]{1,0:T(8,128)S(1)}, f32[48,768]{1,0:T(8,128)}, u32[]{:S(2)}) copy-start(f32[48,768]{1,0:T(8,128)} %param.21) | copy-start | bytes 442372
  55.6 138.9 %copy-start.5 = (f32[768,48]{0,1:T(8,128)S(1)}, f32[768,48]{0,1:T(8,128)}, u32[]{:S(2)}) copy-start(f32[768,48]{0,1:T(8,128)} %param.22) | copy-start | bytes 442372
  55.6 139.6 %copy-start.6 = (f32[48,192]{1,0:T(8,128)S(1)}, f32[48,192]{1,0:T(8,128)}, u32[]{:S(2)}) copy-start(f32[48,192]{1,0:T(8,128)} %param.23) | copy-start | bytes 110596
  55.6 140.2 %copy-start.7 = (f32[192,48]{0,1:T(8,128)S(1)}, f32[192,48]{0,1:T(8,128)}, u32[]{:S(2)}) copy-start(f32[192,48]{0,1:T(8,128)} %param.26) | copy-start | bytes 110596
  55.7 140.8 %copy-start.8 = (f32[48,192]{1,0:T(8,128)S(1)}, f32[48,192]{1,0:T(8,128)}, u32[]{:S(2)}) copy-start(f32[48,192]{1,0:T(8,128)} %param.25) | copy-start | bytes 110596
  55.7 140.8 %copy-start.9 = (f32[48,192]{1,0:T(8,128)S(1)}, f32[48,192]{1,0:T(8,128)}, u32[]{:S(2)}) copy-start(f32[48,192]{1,0:T(8,128)} %param.24) | copy-start | bytes 110596
  55.7 185.1 %all-gather.2.cloned.1.call-start = ((), (), s32[]{:S(2)}) async-start(), calls=%async_computation | async-start | bytes 3969024 | tf_op jit(solution)/shard_map/all_gather | solution.py:32
Sparse Core Ops, SparseCore 0:
  55.8 133.6 all-reduce.3
  198.1 42.6 all-gather.1
where the time goes:
time: 259 us
  waiting for transfers between devices  175 us (68%)
  local copies, waits for them, and re-layouts  63.4 us (24%)
  between operations  14.9 us (6%)
  other arithmetic  5.71 us (2%)
    unnamed x3, waiting for transfers between devices  132 us
    all_gather x1, waiting for transfers between devices, rows_first(): out, at, finished = (lax.all_gather(both, axis, axis=0, tiled=True), 0, [])  42.8 us
    unnamed x43, local copies, waits for them, and re-layouts  20.1 us
    reshape x2, local copies, waits for them, and re-layouts, sum_together(): lines = jnp.concatenate([b.reshape(size, -1) for b in parts], axis=1)  10.8 us
    pad x1, local copies, waits for them, and re-layouts, sum_together(): jnp.pad(lines, ((0, 0), (0, width * 128 - lines.shape[1]))).reshape(-1, 128)  6.35 us
    transpose x2, local copies, waits for them, and re-layouts, split_up(): return jnp.moveaxis(parts, dim, 0)  5.77 us
    reshape x1, local copies, waits for them, and re-layouts, sum_together(): jnp.pad(lines, ((0, 0), (0, width * 128 - lines.shape[1]))).reshape(-1, 128)  5.49 us
    another operation x4, local copies, waits for them, and re-layouts, sum_together(): lines = jnp.concatenate([b.reshape(size, -1) for b in parts], axis=1)  5.22 us
  transfers between devices with their start and end apart: 2, of which 2 were waited for; matrix products, arithmetic and copies ran while one was open for 0% of the time, Pallas kernels for 0%

commit v1 on v0

v1 whole, which is shorter than its diff:
```python
import jax
import jax.numpy as jnp
from jax import lax
from jax.experimental import pallas as pl
from jax.experimental.pallas import tpu as pltpu
from jax.sharding import PartitionSpec as P

learn_rate = 0.3

ROWS = (440, 432)
CUT = 224
GROUPS = ((0, 1, 2, 6, 7), (3, 5), (4,))
f32, bf16 = jnp.float32, jnp.bfloat16
whole = pl.BlockSpec(memory_space=pltpu.VMEM)
scalars = pl.BlockSpec(memory_space=pltpu.SMEM)


def kernel(body, out_shape, in_specs, scratch=()):
    return pl.pallas_call(
        body,
        out_shape=out_shape,
        in_specs=in_specs,
        out_specs=[whole] * len(out_shape),
        scratch_shapes=scratch,
        compiler_params=pltpu.CompilerParams(vmem_limit_bytes=24 << 20),
    )


def three_blocks(a, b):
    tail = jnp.concatenate([a[:, 128:192], b[:, 128:192]], axis=1)
    return a[:, :128], tail, b[:, :128]


def turn(source, target):
    for j in range(6):
        lanes = slice(128 * j, 128 * j + 128)
        target[lanes, :128] = source[0, :128, lanes].T
        rest = jnp.concatenate([source[0, 128:192, lanes], jnp.zeros((64, 128), f32)], axis=0)
        target[lanes, 128:] = rest.T


def chunks(at):
    for k in range(8):
        for shift in (0, 1):
            yield k, shift, 2 * ((at[0] + k) % 8) + (at[1] + shift) % 2


def pack_first_body(at, up, query, key, norm, mine, theirs, q, k_, rows16):
    turn(query, q)
    turn(key, k_)
    rows16[...] = jnp.zeros((16, 128), f32)
    for r in range(16):
        rows16[r : r + 1, :48] = norm[:, 48 * r : 48 * r + 48]
    for k, shift, r in chunks(at):
        out = (mine, theirs)[shift]
        rows = pl.ds(pl.multiple_of(48 * r, 8), 48)
        for j in range(6):
            out[k, 48 * j : 48 * j + 48, :] = up[0, rows, 128 * j : 128 * j + 128]
        for j, block in enumerate(three_blocks(q[rows, :], k_[rows, :])):
            out[k, 288 + 48 * j : 336 + 48 * j, :] = block
        out[k, 432:440, :] = jnp.broadcast_to(rows16[pl.ds(r, 1), :], (8, 128))


def pack_second_body(at, down, value, mixed, mine, theirs, turned, v, m):
    for i in range(6):
        for j in range(6):
            block = down[0, 128 * i : 128 * i + 128, 128 * j : 128 * j + 128]
            turned[128 * j : 128 * j + 128, 128 * i : 128 * i + 128] = block.T
    turn(value, v)
    turn(mixed, m)
    for k, shift, r in chunks(at):
        out = (mine, theirs)[shift]
        rows = pl.ds(pl.multiple_of(48 * r, 8), 48)
        for j in range(6):
            out[k, 48 * j : 48 * j + 48, :] = turned[rows, 128 * j : 128 * j + 128]
        for j, block in enumerate(three_blocks(v[rows, :], m[rows, :])):
            out[k, 288 + 48 * j : 336 + 48 * j, :] = block


def pack_first(at, up, query, key, norm):
    return kernel(
        pack_first_body, [jax.ShapeDtypeStruct((8, 440, 128), f32)] * 2, [scalars] + [whole] * 4,
        [pltpu.VMEM((768, 256), f32)] * 2 + [pltpu.VMEM((16, 128), f32)],
    )(at, up, query, key, norm)


def pack_second(at, down, value, mixed):
    return kernel(
        pack_second_body, [jax.ShapeDtypeStruct((8, 432, 128), f32)] * 2, [scalars] + [whole] * 3,
        [pltpu.VMEM((768, 768), f32)] + [pltpu.VMEM((768, 256), f32)] * 2,
    )(at, down, value, mixed)


def pack_params_body(up, down, query, key, value, mixed, norm, first, second):
    for big, a, b, out in ((up, query, key, first), (down, value, mixed, second)):
        for j in range(6):
            out[48 * j : 48 * j + 48, :] = big[:, 128 * j : 128 * j + 128]
        for j, block in enumerate(three_blocks(a[...], b[...])):
            out[288 + 48 * j : 336 + 48 * j, :] = block
    first[432:440, :] = jnp.zeros((8, 128), f32)
    first[432:433, :48] = norm[...]


def unpack_next_body(first, second, up, down, query, key, value, mixed, norm):
    for new, big, a, b in ((first, up, query, key), (second, down, value, mixed)):
        for j in range(6):
            big[:, 128 * j : 128 * j + 128] = new[48 * j : 48 * j + 48, :]
        tail = new[336:384, :]
        a[:, :128] = new[288:336, :]
        a[:, 128:] = tail[:, :64]
        b[:, :128] = new[384:432, :]
        b[:, 128:] = tail[:, 64:]
    norm[...] = first[432:433, :48]


def pieces(at, refs, rows):
    for shift in (0, 1):
        for ref, ks in zip(refs[3 * shift : 3 * shift + 3], GROUPS):
            for i, k in enumerate(ks):
                r = 2 * ((at[0] + k) % 8) + (at[1] + shift) % 2
                yield r, lambda lo, hi, ref=ref, base=i * rows: ref[base + lo : base + hi, :]


def put_pair(rows, read, a, b):
    first, tail, second = (read(288 + 48 * j, 336 + 48 * j) for j in range(3))
    a[rows, :128] = first
    a[rows, 128:192] = tail[:, :64]
    b[rows, :128] = second
    b[rows, 128:192] = tail[:, 64:]


def turn_back(source, target):
    for j in range(6):
        lanes = slice(128 * j, 128 * j + 128)
        target[:128, lanes] = source[lanes, :128].T
        target[128:, lanes] = source[lanes, 128:].T[:64]


def unpack_first_body(at, *refs):
    up, query, key, norm, q, k_, rows16 = refs[6:]
    for r, read in pieces(at, refs, 440):
        rows = pl.ds(pl.multiple_of(48 * r, 16), 48)
        for j in range(6):
            up[rows, 128 * j : 128 * j + 128] = read(48 * j, 48 * j + 48)
        put_pair(rows, read, q, k_)
        rows16[pl.ds(r, 1), :] = read(432, 440)[:1].astype(f32)
    turn_back(q, query)
    turn_back(k_, key)
    for r in range(16):
        norm[:, 48 * r : 48 * r + 48] = rows16[r : r + 1, :48]


def unpack_second_body(at, *refs):
    down, value, mixed, turned, v, m = refs[6:]
    for r, read in pieces(at, refs, 432):
        rows = pl.ds(pl.multiple_of(48 * r, 16), 48)
        for j in range(6):
            turned[rows, 128 * j : 128 * j + 128] = read(48 * j, 48 * j + 48)
        put_pair(rows, read, v, m)
    for i in range(6):
        for j in range(6):
            block = turned[128 * i : 128 * i + 128, 128 * j : 128 * j + 128]
            down[128 * j : 128 * j + 128, 128 * i : 128 * i + 128] = block.T
    turn_back(v, value)
    turn_back(m, mixed)


def shards(
    slope_up, slope_down, slope_query, slope_key, slope_value, slope_mixed, slope_norm,
    param_up, param_down, param_query, param_key, param_value, param_mixed, param_norm,
):
    n = lax.axis_size("replica")
    chips = n // 2
    me = lax.axis_index("replica")
    at = jnp.stack([me // 2, me % 2]).astype(jnp.int32)
    partner = [(2 * i + k, 2 * i + 1 - k) for i in range(chips) for k in range(2)]
    right = [(2 * i + k, 2 * ((i + 1) % chips) + k) for i in range(chips) for k in range(2)]
    left = [(d, s) for s, d in right]
    rate = learn_rate * n ** (-0.5)
    back = lambda a: jnp.swapaxes(a, -1, -2)

    def send(a, pairs):
        return lax.ppermute(a, "replica", pairs)

    packed = pack_first(at, slope_up, back(slope_query), back(slope_key), slope_norm), pack_second(
        at, slope_down, back(slope_value), slope_mixed
    )
    first, second = kernel(
        pack_params_body, [jax.ShapeDtypeStruct((r, 128), f32) for r in ROWS], [whole] * 7
    )(param_up, back(param_down), param_query, param_key, param_value, back(param_mixed), param_norm.reshape(1, 48))

    news, gots, others = [], [], []
    for (mine, theirs), p in zip(packed, (first, second)):
        pair = send(theirs, partner)
        start = lax.optimization_barrier(mine[4] + pair[4])
        rest = lax.optimization_barrier(tuple(mine[k] + pair[k] for k in range(8) if k != 4))
        own = [*rest[:4], start, *rest[4:]]
        ab = lambda a, b: (send(a, right), send(b, left))
        a, b = ab(own[4][:CUT], own[4][CUT:])
        a = jnp.concatenate([a + own[3][:CUT], own[3][CUT:]])
        b = jnp.concatenate([own[5][:CUT], b + own[5][CUT:]])
        for k in (3, 2, 1):
            a, b = ab(a, b)
            if k > 1:
                a, b = a + own[k - 1], b + own[9 - k]
        new = p - rate * (a + b + own[0])
        news.append(new)
        h = new.astype(bf16)
        got = {0: h}
        a, b = h, h
        for k in range(1, 4):
            a, b = ab(a, b)
            got[8 - k], got[k] = a, b
        got[4] = jnp.concatenate(ab(a[:CUT], b[CUT:]))
        groups = [jnp.concatenate([got[k] for k in ks]) for ks in GROUPS]
        gots.append(groups)
        others.append([send(g, partner) for g in groups])

    shapes = ((48, 768), (48, 768), (48, 192), (48, 192), (48, 192), (48, 192), (1, 48))
    nexts = kernel(unpack_next_body, [jax.ShapeDtypeStruct(x, f32) for x in shapes], [whole] * 2)(*news)
    shape = lambda *x: jax.ShapeDtypeStruct(x, bf16)
    up, query, key, norm = kernel(
        unpack_first_body, [shape(768, 768), shape(192, 768), shape(192, 768), jax.ShapeDtypeStruct((1, 768), f32)],
        [scalars] + [whole] * 6, [pltpu.VMEM((768, 256), bf16)] * 2 + [pltpu.VMEM((16, 128), f32)],
    )(at, *gots[0], *others[0])
    down, value, mixed = kernel(
        unpack_second_body, [shape(768, 768), shape(192, 768), shape(192, 768)],
        [scalars] + [whole] * 6, [pltpu.VMEM((768, 768), bf16)] + [pltpu.VMEM((768, 256), bf16)] * 2,
    )(at, *gots[1], *others[1])
    nup, ndown, nquery, nkey, nvalue, nmixed, nnorm = nexts
    return (
        up, down, back(query), back(key), back(value), mixed, norm.reshape(768).astype(bf16),
        nup, back(ndown), nquery, nkey, nvalue, back(nmixed), nnorm.reshape(48),
    )


def solution(mesh):
    rep = ("unit", "replica")
    um = ("unit", "model")
    args = [P(rep, None, "model"), P(rep, "model", None)] + [P(rep, None, "model")] * 3 + [P(rep, "model", None), P(rep, None)]
    nxt = [P(rep, "model"), P(um, "replica")] + [P(rep, "model")] * 3 + [P(um, "replica"), P(rep)]
    half = [P("unit", "model"), P(um, None)] + [P("unit", "model")] * 3 + [P(um, None), P("unit")]
    return jax.shard_map(shards, mesh=mesh, in_specs=tuple(args + nxt), out_specs=tuple(half + nxt), check_vma=False)
```

time: 259 us -> 96.7 us (0.37)
  waiting for transfers between devices: 175 us -> 18.6 us
  starting transfers between devices: 0.08 us -> 62 us
  local copies, waits for them, and re-layouts: 63.4 us -> 4.16 us
  between operations: 14.9 us -> 1.25 us
  Pallas kernels: 0 us -> 8.76 us
  other arithmetic: 5.71 us -> 1.71 us
    unnamed x3 -> x0, waiting for transfers between devices: 132 us -> none
    ppermute x0 -> x40, starting transfers between devices: none -> 62 us  [send(): return lax.ppermute(a, 'replica', pairs)]
    all_gather x1 -> x0, waiting for transfers between devices: 42.8 us -> none  [rows_first(): out, at, finished = (lax.all_gather(both, axis, axis=0, tiled=True), 0, [])]
    ppermute x0 -> x40, waiting for transfers between devices: none -> 18.6 us  [send(): return lax.ppermute(a, 'replica', pairs)]
    reshape x5 -> x0, local copies, waits for them, and re-layouts: 17.4 us -> none  [the longest x2 10.8 us: sum_together(): lines = jnp.concatenate([b.reshape(size, -1) for b in parts], axis=1)]
    unnamed x43 -> x38, local copies, waits for them, and re-layouts: 20.1 us -> 3.98 us
    transpose x4 -> x0, local copies, waits for them, and re-layouts: 10.5 us -> none  [the longest x2 5.77 us: split_up(): return jnp.moveaxis(parts, dim, 0)]
    pallas_call x0 -> x6, Pallas kernels: none -> 8.76 us  [the longest x1 2.44 us: shards(): kernel(unpack_second_body, [shape(768, 768), shape(192, 768), shape(192,...]
  transfers between devices with their start and end apart: 2 -> 40, of which waited for: 2 -> 13; matrix products, arithmetic and copies ran while one was open for 0% -> 1% of each run, Pallas kernels for 0% -> 5%
where the time goes in v1:
time: 96.7 us; the launch traced here: 96.5 us
  starting transfers between devices  62 us (64%)
  waiting for transfers between devices  18.6 us (19%)
  Pallas kernels  8.76 us (9%)
  local copies, waits for them, and re-layouts  4.16 us (4%)
  other arithmetic  1.71 us (2%)
  between operations  1.25 us (1%)
    ppermute x40, starting transfers between devices, send(): return lax.ppermute(a, 'replica', pairs)  62 us
    ppermute x40, waiting for transfers between devices, send(): return lax.ppermute(a, 'replica', pairs)  18.6 us
    unnamed x38, local copies, waits for them, and re-layouts  3.98 us
    pallas_call x1, Pallas kernels, shards(): kernel(unpack_second_body, [shape(768, 768), shape(192, 768), shape(192,...  2.44 us
    pallas_call x1, Pallas kernels, shards(): kernel(unpack_first_body, [shape(768, 768), shape(192, 768), shape(192, 7...  2.2 us
    pallas_call x1, Pallas kernels, pack_second(): kernel(pack_second_body, [jax.ShapeDtypeStruct((8, 432, 128), f32)] * 2,...  1.95 us
  transfers between devices with their start and end apart: 40, of which 13 were waited for; matrix products, arithmetic and copies ran while one was open for 1% of the time, Pallas kernels for 5%

profile of v1, /device:TPU:1, one launch (start us, length us, event | category | flops | bytes accessed | tf_op | source)
XLA Modules:
  0.0 96.5 jit_solution(3606835941501890150)
XLA Ops:
  0.8 1.7 %copy-done = f32[1,768,768]{2,1,0:T(8,128)S(1)} copy-done((f32[1,768,768]{2,1,0:T(8,128)S(1)}, f32[1,768,768]{2,1,0:T(8,128)}, u32[]{:S(2)}) %copy-start) | copy-done | bytes 2359320
  4.6 2.0 %shard_map.248 = (f32[8,432,128]{2,1,0:T(8,128)S(1)}, f32[8,432,128]{2,1,0:T(8,128)S(1)}) custom-call(s32[2]{0:T(128)S(1)} %pad_add_fusion.at, f32[1,768,768]{2,1,0:T(8,128)S(1)} %copy-done, f32[1,192,768]{2,1,0:T(8,128)S(1)} %bitcast.48, f32[1,192,768]{2,1,0:T(8,128)S(1)} %copy-done.5), custom_call_target="tpu_custom_call" | custom-call | tf_op jit(solution)/shard_map/pallas_call | solution.py:88
  6.5 3.3 %collective-permute-start.20 = (f32[8,432,128]{2,1,0:T(8,128)S(1)}, f32[8,432,128]{2,1,0:T(8,128)S(1)}, u32[]{:S(2)}, u32[]{:S(2)}) collective-permute-start(f32[8,432,128]{2,1,0:T(8,128)S(1)} %get-tuple-element.61), channel_id=1, source_target_pairs={{0,4},{4,0},{8,12},{12,8},{16,20},{20,16},{24,28},{28,24},{32,36},... | collective-permute-start | bytes 5308424 | tf_op jit(solution)/shard_map/ppermute | solution.py:183
  9.8 1.3 %shard_map.246 = (f32[8,440,128]{2,1,0:T(8,128)S(1)}, f32[8,440,128]{2,1,0:T(8,128)S(1)}) custom-call(s32[2]{0:T(128)S(1)} %pad_add_fusion.at, f32[1,768,768]{2,1,0:T(8,128)S(1)} %copy-done.1, f32[1,192,768]{2,1,0:T(8,128)S(1)} %bitcast.46, f32[1,192,768]{2,1,0:T(8,128)S(1)} %bitcast.47, f32[1,768]{1,0:T(1,128)S(1)} %copy-done.12), custom_call_target="tpu_custom_call" | custom-call | tf_op jit(solution)/shard_map/pallas_call | solution.py:81
  11.2 1.9 %collective-permute-done.20 = f32[8,432,128]{2,1,0:T(8,128)S(1)} collective-permute-done((f32[8,432,128]{2,1,0:T(8,128)S(1)}, f32[8,432,128]{2,1,0:T(8,128)S(1)}, u32[]{:S(2)}, u32[]{:S(2)}) %collective-permute-start.20) | collective-permute-done | bytes 1769504 | tf_op jit(solution)/shard_map/ppermute | solution.py:183
  13.5 3.9 %collective-permute-start.25 = (f32[208,128]{1,0:T(8,128)S(1)}, f32[208,128]{1,0:T(8,128)S(1)}, u32[]{:S(2)}, u32[]{:S(2)}) collective-permute-start(f32[208,128]{1,0:T(8,128)S(1)} %slice.213), channel_id=1, source_target_pairs={{8,0},{12,4},{16,8},{20,12},{24,16},{28,20},{32,24},{36,28},{40,32... | collective-permute-start | bytes 319496 | tf_op jit(solution)/shard_map/ppermute | solution.py:183
  17.8 2.7 %collective-permute-start.5 = (f32[216,128]{1,0:T(8,128)S(1)}, f32[216,128]{1,0:T(8,128)S(1)}, u32[]{:S(2)}, u32[]{:S(2)}) collective-permute-start(f32[216,128]{1,0:T(8,128)S(1)} %slice.201), channel_id=1, source_target_pairs={{8,0},{12,4},{16,8},{20,12},{24,16},{28,20},{32,24},{36,28},{40,32... | collective-permute-start | bytes 331784 | tf_op jit(solution)/shard_map/ppermute | solution.py:183
  20.7 2.7 %collective-permute-start.26 = (f32[432,128]{1,0:T(8,128)S(1)}, f32[432,128]{1,0:T(8,128)S(1)}, u32[]{:S(2)}, u32[]{:S(2)}) collective-permute-start(f32[432,128]{1,0:T(8,128)S(1)} %pad_maximum_fusion.3), channel_id=1, source_target_pairs={{8,0},{12,4},{16,8},{20,12},{24,16},{28,20},{32,24},{36,28},{40,32... | collective-permute-start | bytes 663560 | tf_op jit(solution)/shard_map/ppermute | solution.py:183
  23.6 2.7 %collective-permute-start.6 = (f32[440,128]{1,0:T(8,128)S(1)}, f32[440,128]{1,0:T(8,128)S(1)}, u32[]{:S(2)}, u32[]{:S(2)}) collective-permute-start(f32[440,128]{1,0:T(8,128)S(1)} %pad_maximum_fusion.1), channel_id=1, source_target_pairs={{8,0},{12,4},{16,8},{20,12},{24,16},{28,20},{32,24},{36,28},{40,32... | collective-permute-start | bytes 675848 | tf_op jit(solution)/shard_map/ppermute | solution.py:183
  26.8 3.5 %collective-permute-start.27 = (f32[432,128]{1,0:T(8,128)S(1)}, f32[432,128]{1,0:T(8,128)S(1)}, u32[]{:S(2)}, u32[]{:S(2)}) collective-permute-start(f32[432,128]{1,0:T(8,128)S(1)} %add.194), channel_id=1, source_target_pairs={{8,0},{12,4},{16,8},{20,12},{24,16},{28,20},{32,24},{36,28},{40,32... | collective-permute-start | bytes 663560 | tf_op jit(solution)/shard_map/ppermute | solution.py:183
  30.4 1.2 %collective-permute-done.6 = f32[440,128]{1,0:T(8,128)S(1)} collective-permute-done((f32[440,128]{1,0:T(8,128)S(1)}, f32[440,128]{1,0:T(8,128)S(1)}, u32[]{:S(2)}, u32[]{:S(2)}) %collective-permute-start.6) | collective-permute-done | bytes 225312 | tf_op jit(solution)/shard_map/ppermute | solution.py:183
  31.7 3.5 %collective-permute-start.7 = (f32[440,128]{1,0:T(8,128)S(1)}, f32[440,128]{1,0:T(8,128)S(1)}, u32[]{:S(2)}, u32[]{:S(2)}) collective-permute-start(f32[440,128]{1,0:T(8,128)S(1)} %add.170), channel_id=1, source_target_pairs={{8,0},{12,4},{16,8},{20,12},{24,16},{28,20},{32,24},{36,28},{40,32... | collective-permute-start | bytes 675848 | tf_op jit(solution)/shard_map/ppermute | solution.py:183
  36.3 3.5 %collective-permute-start.28 = (f32[432,128]{1,0:T(8,128)S(1)}, f32[432,128]{1,0:T(8,128)S(1)}, u32[]{:S(2)}, u32[]{:S(2)}) collective-permute-start(f32[432,128]{1,0:T(8,128)S(1)} %add.195), channel_id=1, source_target_pairs={{8,0},{12,4},{16,8},{20,12},{24,16},{28,20},{32,24},{36,28},{40,32... | collective-permute-start | bytes 663560 | tf_op jit(solution)/shard_map/ppermute | solution.py:183
  41.1 3.5 %collective-permute-start.8 = (f32[440,128]{1,0:T(8,128)S(1)}, f32[440,128]{1,0:T(8,128)S(1)}, u32[]{:S(2)}, u32[]{:S(2)}) collective-permute-start(f32[440,128]{1,0:T(8,128)S(1)} %add.171), channel_id=1, source_target_pairs={{8,0},{12,4},{16,8},{20,12},{24,16},{28,20},{32,24},{36,28},{40,32... | collective-permute-start | bytes 675848 | tf_op jit(solution)/shard_map/ppermute | solution.py:183
  45.8 3.1 %collective-permute-done.24 = f32[432,128]{1,0:T(8,128)S(1)} collective-permute-done((f32[432,128]{1,0:T(8,128)S(1)}, f32[432,128]{1,0:T(8,128)S(1)}, u32[]{:S(2)}, u32[]{:S(2)}) %collective-permute-start.24) | collective-permute-done | bytes 221216 | tf_op jit(solution)/shard_map/ppermute | solution.py:183
  49.1 2.7 %collective-permute-start.29 = (bf16[432,128]{1,0:T(8,128)(2,1)S(1)}, bf16[432,128]{1,0:T(8,128)(2,1)S(1)}, u32[]{:S(2)}, u32[]{:S(2)}) collective-permute-start(bf16[432,128]{1,0:T(8,128)(2,1)S(1)} %get-tuple-element.83), channel_id=1, source_target_pairs={{8,0},{12,4},{16,8},{20,12},{24,16},{28,20},{32,24},{36,28},{40,32... | collective-permute-start | bytes 331784 | tf_op jit(solution)/shard_map/ppermute | solution.py:183
  51.8 2.0 %collective-permute-done.4 = f32[440,128]{1,0:T(8,128)S(1)} collective-permute-done((f32[440,128]{1,0:T(8,128)S(1)}, f32[440,128]{1,0:T(8,128)S(1)}, u32[]{:S(2)}, u32[]{:S(2)}) %collective-permute-start.4) | collective-permute-done | bytes 225312 | tf_op jit(solution)/shard_map/ppermute | solution.py:183
  53.9 2.7 %collective-permute-start.9 = (bf16[440,128]{1,0:T(8,128)(2,1)S(1)}, bf16[440,128]{1,0:T(8,128)(2,1)S(1)}, u32[]{:S(2)}, u32[]{:S(2)}) collective-permute-start(bf16[440,128]{1,0:T(8,128)(2,1)S(1)} %get-tuple-element.86), channel_id=1, source_target_pairs={{8,0},{12,4},{16,8},{20,12},{24,16},{28,20},{32,24},{36,28},{40,32... | collective-permute-start | bytes 337928 | tf_op jit(solution)/shard_map/ppermute | solution.py:183
  56.6 2.7 %collective-permute-start.30 = (bf16[432,128]{1,0:T(8,128)(2,1)S(1)}, bf16[432,128]{1,0:T(8,128)(2,1)S(1)}, u32[]{:S(2)}, u32[]{:S(2)}) collective-permute-start(bf16[432,128]{1,0:T(8,128)(2,1)S(1)} %collective-permute-done.29), channel_id=1, source_target_pairs={{8,0},{12,4},{16,8},{20,12},{24,16},{28,20},{32,24},{36,28},{40,32... | collective-permute-start | bytes 331784 | tf_op jit(solution)/shard_map/ppermute | solution.py:183
  59.4 2.7 %collective-permute-start.10 = (bf16[440,128]{1,0:T(8,128)(2,1)S(1)}, bf16[440,128]{1,0:T(8,128)(2,1)S(1)}, u32[]{:S(2)}, u32[]{:S(2)}) collective-permute-start(bf16[440,128]{1,0:T(8,128)(2,1)S(1)} %collective-permute-done.9), channel_id=1, source_target_pairs={{8,0},{12,4},{16,8},{20,12},{24,16},{28,20},{32,24},{36,28},{40,32... | collective-permute-start | bytes 337928 | tf_op jit(solution)/shard_map/ppermute | solution.py:183
  62.2 5.8 %collective-permute-start.37 = (bf16[2160,128]{1,0:T(8,128)(2,1)S(1)}, bf16[2160,128]{1,0:T(8,128)(2,1)S(1)}, u32[]{:S(2)}, u32[]{:S(2)}) collective-permute-start(bf16[2160,128]{1,0:T(8,128)(2,1)S(1)} %constant_dynamic-update-slice_fusion.9.refs_0_), channel_id=1, source_target_pairs={{0,4},{4,0},{8,12},{12,8},{16,20},{20,16},{24,28},{28,24},{32,36},... | collective-permute-start | bytes 1658888 | tf_op jit(solution)/shard_map/ppermute | solution.py:183
  68.0 2.7 %collective-permute-start.33 = (bf16[432,128]{1,0:T(8,128)(2,1)S(1)}, bf16[432,128]{1,0:T(8,128)(2,1)S(1)}, u32[]{:S(2)}, u32[]{:S(2)}) collective-permute-start(bf16[432,128]{1,0:T(8,128)(2,1)S(1)} %collective-permute-done.30), channel_id=1, source_target_pairs={{8,0},{12,4},{16,8},{20,12},{24,16},{28,20},{32,24},{36,28},{40,32... | collective-permute-start | bytes 331784 | tf_op jit(solution)/shard_map/ppermute | solution.py:183
  71.7 2.0 %collective-permute-done.34 = bf16[432,128]{1,0:T(8,128)(2,1)S(1)} collective-permute-done((bf16[432,128]{1,0:T(8,128)(2,1)S(1)}, bf16[432,128]{1,0:T(8,128)(2,1)S(1)}, u32[]{:S(2)}, u32[]{:S(2)}) %collective-permute-start.34) | collective-permute-done | bytes 110624 | tf_op jit(solution)/shard_map/ppermute | solution.py:183
  73.7 1.1 %collective-permute-start.13 = (bf16[440,128]{1,0:T(8,128)(2,1)S(1)}, bf16[440,128]{1,0:T(8,128)(2,1)S(1)}, u32[]{:S(2)}, u32[]{:S(2)}) collective-permute-start(bf16[440,128]{1,0:T(8,128)(2,1)S(1)} %collective-permute-done.10), channel_id=1, source_target_pairs={{8,0},{12,4},{16,8},{20,12},{24,16},{28,20},{32,24},{36,28},{40,32... | collective-permute-start | bytes 337928 | tf_op jit(solution)/shard_map/ppermute | solution.py:183
  75.3 2.3 %collective-permute-done.13 = bf16[440,128]{1,0:T(8,128)(2,1)S(1)} collective-permute-done((bf16[440,128]{1,0:T(8,128)(2,1)S(1)}, bf16[440,128]{1,0:T(8,128)(2,1)S(1)}, u32[]{:S(2)}, u32[]{:S(2)}) %collective-permute-start.13) | collective-permute-done | bytes 112672 | tf_op jit(solution)/shard_map/ppermute | solution.py:183
  77.6 2.0 %collective-permute-start.36 = (bf16[208,128]{1,0:T(8,128)(2,1)S(1)}, bf16[208,128]{1,0:T(8,128)(2,1)S(1)}, u32[]{:S(2)}, u32[]{:S(2)}) collective-permute-start(bf16[208,128]{1,0:T(8,128)(2,1)S(1)} %slice.215), channel_id=1, source_target_pairs={{8,0},{12,4},{16,8},{20,12},{24,16},{28,20},{32,24},{36,28},{40,32... | collective-permute-start | bytes 159752 | tf_op jit(solution)/shard_map/ppermute | solution.py:183
  79.6 2.5 %collective-permute-start.38 = (bf16[864,128]{1,0:T(8,128)(2,1)S(1)}, bf16[864,128]{1,0:T(8,128)(2,1)S(1)}, u32[]{:S(2)}, u32[]{:S(2)}) collective-permute-start(bf16[864,128]{1,0:T(8,128)(2,1)S(1)} %constant_dynamic-update-slice_fusion.14.refs_1_), channel_id=1, source_target_pairs={{0,4},{4,0},{8,12},{12,8},{16,20},{20,16},{24,28},{28,24},{32,36},... | collective-permute-start | bytes 663560 | tf_op jit(solution)/shard_map/ppermute | solution.py:183
  82.3 2.7 %collective-permute-start.16 = (bf16[216,128]{1,0:T(8,128)(2,1)S(1)}, bf16[216,128]{1,0:T(8,128)(2,1)S(1)}, u32[]{:S(2)}, u32[]{:S(2)}) collective-permute-start(bf16[216,128]{1,0:T(8,128)(2,1)S(1)} %slice.203), channel_id=1, source_target_pairs={{8,0},{12,4},{16,8},{20,12},{24,16},{28,20},{32,24},{36,28},{40,32... | collective-permute-start | bytes 165896 | tf_op jit(solution)/shard_map/ppermute | solution.py:183
  85.0 1.9 %collective-permute-done.15 = bf16[224,128]{1,0:T(8,128)(2,1)S(1)} collective-permute-done((bf16[224,128]{1,0:T(8,128)(2,1)S(1)}, bf16[224,128]{1,0:T(8,128)(2,1)S(1)}, u32[]{:S(2)}, u32[]{:S(2)}) %collective-permute-start.15) | collective-permute-done | bytes 57376 | tf_op jit(solution)/shard_map/ppermute | solution.py:183
  87.8 1.4 %collective-permute-start.39 = (bf16[432,128]{1,0:T(8,128)(2,1)S(1)}, bf16[432,128]{1,0:T(8,128)(2,1)S(1)}, u32[]{:S(2)}, u32[]{:S(2)}) collective-permute-start(bf16[432,128]{1,0:T(8,128)(2,1)S(1)} %constant_dynamic-update-slice_fusion.16.refs_2_), channel_id=1, source_target_pairs={{0,4},{4,0},{8,12},{12,8},{16,20},{20,16},{24,28},{28,24},{32,36},... | collective-permute-start | bytes 331784 | tf_op jit(solution)/shard_map/ppermute | solution.py:183
  91.2 2.4 %shard_map.249 = (bf16[768,768]{1,0:T(8,128)(2,1)}, bf16[192,768]{1,0:T(8,128)(2,1)}, bf16[192,768]{1,0:T(8,128)(2,1)}) custom-call(s32[2]{0:T(128)S(1)} %pad_add_fusion.at, bf16[2160,128]{1,0:T(8,128)(2,1)S(1)} %constant_dynamic-update-slice_fusion.9.refs_0_, bf16[864,128]{1,0:T(8,128)(2,1)S(1)} %constant_dynamic-update-slice_fusion.14.refs_1_, ...), custom_call_target="tpu_custom_call" | custom-call | tf_op jit(solution)/shard_map/pallas_call | solution.py:226
  93.7 2.2 %shard_map.247 = (bf16[768,768]{1,0:T(8,128)(2,1)}, bf16[192,768]{1,0:T(8,128)(2,1)}, bf16[192,768]{1,0:T(8,128)(2,1)}, f32[1,768]{1,0:T(1,128)S(1)}) custom-call(s32[2]{0:T(128)S(1)} %pad_add_fusion.at, bf16[2200,128]{1,0:T(8,128)(2,1)S(1)} %constant_dynamic-update-slice_fusion.refs_0_, bf16[880,128]{1,0:T(8,128)(2,1)S(1)} %constant_dynamic-update-slice_fusion.5.refs_1_, ...), custom_call_target="tpu_custom_call" | custom-call | tf_op jit(solution)/shard_map/pallas_call | solution.py:222
  (132 shorter events, 13.2 us)
Async XLA Ops:
  6.5 6.6 %collective-permute-start.20 = (f32[8,432,128]{2,1,0:T(8,128)S(1)}, f32[8,432,128]{2,1,0:T(8,128)S(1)}, u32[]{:S(2)}, u32[]{:S(2)}) collective-permute-start(f32[8,432,128]{2,1,0:T(8,128)S(1)} %get-tuple-element.61), channel_id=1, source_target_pairs={{0,4},{4,0},{8,12},{12,8},{16,20},{20,16},{24,28},{28,24},{32,36},... | collective-permute-start | bytes 5308424 | tf_op jit(solution)/shard_map/ppermute | solution.py:183
  11.1 6.5 %collective-permute-start = (f32[8,440,128]{2,1,0:T(8,128)S(1)}, f32[8,440,128]{2,1,0:T(8,128)S(1)}, u32[]{:S(2)}, u32[]{:S(2)}) collective-permute-start(f32[8,440,128]{2,1,0:T(8,128)S(1)} %get-tuple-element.50), channel_id=1, source_target_pairs={{0,4},{4,0},{8,12},{12,8},{16,20},{20,16},{24,28},{28,24},{32,36},... | collective-permute-start | bytes 5406728 | tf_op jit(solution)/shard_map/ppermute | solution.py:183
  13.5 7.2 %collective-permute-start.25 = (f32[208,128]{1,0:T(8,128)S(1)}, f32[208,128]{1,0:T(8,128)S(1)}, u32[]{:S(2)}, u32[]{:S(2)}) collective-permute-start(f32[208,128]{1,0:T(8,128)S(1)} %slice.213), channel_id=1, source_target_pairs={{8,0},{12,4},{16,8},{20,12},{24,16},{28,20},{32,24},{36,28},{40,32... | collective-permute-start | bytes 319496 | tf_op jit(solution)/shard_map/ppermute | solution.py:183
  17.4 6.0 %collective-permute-start.21 = (f32[224,128]{1,0:T(8,128)S(1)}, f32[224,128]{1,0:T(8,128)S(1)}, u32[]{:S(2)}, u32[]{:S(2)}) collective-permute-start(f32[224,128]{1,0:T(8,128)S(1)} %slice.205), channel_id=1, source_target_pairs={{0,8},{4,12},{8,16},{12,20},{16,24},{20,28},{24,32},{28,36},{32,40... | collective-permute-start | bytes 344072 | tf_op jit(solution)/shard_map/ppermute | solution.py:183
  17.8 5.8 %collective-permute-start.5 = (f32[216,128]{1,0:T(8,128)S(1)}, f32[216,128]{1,0:T(8,128)S(1)}, u32[]{:S(2)}, u32[]{:S(2)}) collective-permute-start(f32[216,128]{1,0:T(8,128)S(1)} %slice.201), channel_id=1, source_target_pairs={{8,0},{12,4},{16,8},{20,12},{24,16},{28,20},{32,24},{36,28},{40,32... | collective-permute-start | bytes 331784 | tf_op jit(solution)/shard_map/ppermute | solution.py:183
  20.5 5.8 %collective-permute-start.1 = (f32[224,128]{1,0:T(8,128)S(1)}, f32[224,128]{1,0:T(8,128)S(1)}, u32[]{:S(2)}, u32[]{:S(2)}) collective-permute-start(f32[224,128]{1,0:T(8,128)S(1)} %slice.193), channel_id=1, source_target_pairs={{0,8},{4,12},{8,16},{12,20},{16,24},{20,28},{24,32},{28,36},{32,40... | collective-permute-start | bytes 344072 | tf_op jit(solution)/shard_map/ppermute | solution.py:183
  20.7 6.0 %collective-permute-start.26 = (f32[432,128]{1,0:T(8,128)S(1)}, f32[432,128]{1,0:T(8,128)S(1)}, u32[]{:S(2)}, u32[]{:S(2)}) collective-permute-start(f32[432,128]{1,0:T(8,128)S(1)} %pad_maximum_fusion.3), channel_id=1, source_target_pairs={{8,0},{12,4},{16,8},{20,12},{24,16},{28,20},{32,24},{36,28},{40,32... | collective-permute-start | bytes 663560 | tf_op jit(solution)/shard_map/ppermute | solution.py:183
  23.5 6.8 %collective-permute-start.22 = (f32[432,128]{1,0:T(8,128)S(1)}, f32[432,128]{1,0:T(8,128)S(1)}, u32[]{:S(2)}, u32[]{:S(2)}) collective-permute-start(f32[432,128]{1,0:T(8,128)S(1)} %pad_maximum_fusion.2), channel_id=1, source_target_pairs={{0,8},{4,12},{8,16},{12,20},{16,24},{20,28},{24,32},{28,36},{32,40... | collective-permute-start | bytes 663560 | tf_op jit(solution)/shard_map/ppermute | solution.py:183
  23.6 8.1 %collective-permute-start.6 = (f32[440,128]{1,0:T(8,128)S(1)}, f32[440,128]{1,0:T(8,128)S(1)}, u32[]{:S(2)}, u32[]{:S(2)}) collective-permute-start(f32[440,128]{1,0:T(8,128)S(1)} %pad_maximum_fusion.1), channel_id=1, source_target_pairs={{8,0},{12,4},{16,8},{20,12},{24,16},{28,20},{32,24},{36,28},{40,32... | collective-permute-start | bytes 675848 | tf_op jit(solution)/shard_map/ppermute | solution.py:183
  26.4 8.8 %collective-permute-start.2 = (f32[440,128]{1,0:T(8,128)S(1)}, f32[440,128]{1,0:T(8,128)S(1)}, u32[]{:S(2)}, u32[]{:S(2)}) collective-permute-start(f32[440,128]{1,0:T(8,128)S(1)} %pad_maximum_fusion), channel_id=1, source_target_pairs={{0,8},{4,12},{8,16},{12,20},{16,24},{20,28},{24,32},{28,36},{32,40... | collective-permute-start | bytes 675848 | tf_op jit(solution)/shard_map/ppermute | solution.py:183
  26.8 9.5 %collective-permute-start.27 = (f32[432,128]{1,0:T(8,128)S(1)}, f32[432,128]{1,0:T(8,128)S(1)}, u32[]{:S(2)}, u32[]{:S(2)}) collective-permute-start(f32[432,128]{1,0:T(8,128)S(1)} %add.194), channel_id=1, source_target_pairs={{8,0},{12,4},{16,8},{20,12},{24,16},{28,20},{32,24},{36,28},{40,32... | collective-permute-start | bytes 663560 | tf_op jit(solution)/shard_map/ppermute | solution.py:183
  30.4 9.5 %collective-permute-start.23 = (f32[432,128]{1,0:T(8,128)S(1)}, f32[432,128]{1,0:T(8,128)S(1)}, u32[]{:S(2)}, u32[]{:S(2)}) collective-permute-start(f32[432,128]{1,0:T(8,128)S(1)} %add.191), channel_id=1, source_target_pairs={{0,8},{4,12},{8,16},{12,20},{16,24},{20,28},{24,32},{28,36},{32,40... | collective-permute-start | bytes 663560 | tf_op jit(solution)/shard_map/ppermute | solution.py:183
  31.7 9.4 %collective-permute-start.7 = (f32[440,128]{1,0:T(8,128)S(1)}, f32[440,128]{1,0:T(8,128)S(1)}, u32[]{:S(2)}, u32[]{:S(2)}) collective-permute-start(f32[440,128]{1,0:T(8,128)S(1)} %add.170), channel_id=1, source_target_pairs={{8,0},{12,4},{16,8},{20,12},{24,16},{28,20},{32,24},{36,28},{40,32... | collective-permute-start | bytes 675848 | tf_op jit(solution)/shard_map/ppermute | solution.py:183
  35.3 9.4 %collective-permute-start.3 = (f32[440,128]{1,0:T(8,128)S(1)}, f32[440,128]{1,0:T(8,128)S(1)}, u32[]{:S(2)}, u32[]{:S(2)}) collective-permute-start(f32[440,128]{1,0:T(8,128)S(1)} %add.167), channel_id=1, source_target_pairs={{0,8},{4,12},{8,16},{12,20},{16,24},{20,28},{24,32},{28,36},{32,40... | collective-permute-start | bytes 675848 | tf_op jit(solution)/shard_map/ppermute | solution.py:183
  36.3 9.5 %collective-permute-start.28 = (f32[432,128]{1,0:T(8,128)S(1)}, f32[432,128]{1,0:T(8,128)S(1)}, u32[]{:S(2)}, u32[]{:S(2)}) collective-permute-start(f32[432,128]{1,0:T(8,128)S(1)} %add.195), channel_id=1, source_target_pairs={{8,0},{12,4},{16,8},{20,12},{24,16},{28,20},{32,24},{36,28},{40,32... | collective-permute-start | bytes 663560 | tf_op jit(solution)/shard_map/ppermute | solution.py:183
  39.8 9.1 %collective-permute-start.24 = (f32[432,128]{1,0:T(8,128)S(1)}, f32[432,128]{1,0:T(8,128)S(1)}, u32[]{:S(2)}, u32[]{:S(2)}) collective-permute-start(f32[432,128]{1,0:T(8,128)S(1)} %add.192), channel_id=1, source_target_pairs={{0,8},{4,12},{8,16},{12,20},{16,24},{20,28},{24,32},{28,36},{32,40... | collective-permute-start | bytes 663560 | tf_op jit(solution)/shard_map/ppermute | solution.py:183
  41.1 10.6 %collective-permute-start.8 = (f32[440,128]{1,0:T(8,128)S(1)}, f32[440,128]{1,0:T(8,128)S(1)}, u32[]{:S(2)}, u32[]{:S(2)}) collective-permute-start(f32[440,128]{1,0:T(8,128)S(1)} %add.171), channel_id=1, source_target_pairs={{8,0},{12,4},{16,8},{20,12},{24,16},{28,20},{32,24},{36,28},{40,32... | collective-permute-start | bytes 675848 | tf_op jit(solution)/shard_map/ppermute | solution.py:183
  44.7 9.1 %collective-permute-start.4 = (f32[440,128]{1,0:T(8,128)S(1)}, f32[440,128]{1,0:T(8,128)S(1)}, u32[]{:S(2)}, u32[]{:S(2)}) collective-permute-start(f32[440,128]{1,0:T(8,128)S(1)} %add.168), channel_id=1, source_target_pairs={{0,8},{4,12},{8,16},{12,20},{16,24},{20,28},{24,32},{28,36},{32,40... | collective-permute-start | bytes 675848 | tf_op jit(solution)/shard_map/ppermute | solution.py:183
  49.0 7.6 %collective-permute-start.31 = (bf16[432,128]{1,0:T(8,128)(2,1)S(1)}, bf16[432,128]{1,0:T(8,128)(2,1)S(1)}, u32[]{:S(2)}, u32[]{:S(2)}) collective-permute-start(bf16[432,128]{1,0:T(8,128)(2,1)S(1)} %get-tuple-element.83), channel_id=1, source_target_pairs={{0,8},{4,12},{8,16},{12,20},{16,24},{20,28},{24,32},{28,36},{32,40... | collective-permute-start | bytes 331784 | tf_op jit(solution)/shard_map/ppermute | solution.py:183
  49.1 7.5 %collective-permute-start.29 = (bf16[432,128]{1,0:T(8,128)(2,1)S(1)}, bf16[432,128]{1,0:T(8,128)(2,1)S(1)}, u32[]{:S(2)}, u32[]{:S(2)}) collective-permute-start(bf16[432,128]{1,0:T(8,128)(2,1)S(1)} %get-tuple-element.83), channel_id=1, source_target_pairs={{8,0},{12,4},{16,8},{20,12},{24,16},{28,20},{32,24},{36,28},{40,32... | collective-permute-start | bytes 331784 | tf_op jit(solution)/shard_map/ppermute | solution.py:183
  53.8 5.5 %collective-permute-start.11 = (bf16[440,128]{1,0:T(8,128)(2,1)S(1)}, bf16[440,128]{1,0:T(8,128)(2,1)S(1)}, u32[]{:S(2)}, u32[]{:S(2)}) collective-permute-start(bf16[440,128]{1,0:T(8,128)(2,1)S(1)} %get-tuple-element.86), channel_id=1, source_target_pairs={{0,8},{4,12},{8,16},{12,20},{16,24},{20,28},{24,32},{28,36},{32,40... | collective-permute-start | bytes 337928 | tf_op jit(solution)/shard_map/ppermute | solution.py:183
  56.6 5.5 %collective-permute-start.32 = (bf16[432,128]{1,0:T(8,128)(2,1)S(1)}, bf16[432,128]{1,0:T(8,128)(2,1)S(1)}, u32[]{:S(2)}, u32[]{:S(2)}) collective-permute-start(bf16[432,128]{1,0:T(8,128)(2,1)S(1)} %collective-permute-done.31), channel_id=1, source_target_pairs={{0,8},{4,12},{8,16},{12,20},{16,24},{20,28},{24,32},{28,36},{32,40... | collective-permute-start | bytes 331784 | tf_op jit(solution)/shard_map/ppermute | solution.py:183
  59.4 11.3 %collective-permute-start.12 = (bf16[440,128]{1,0:T(8,128)(2,1)S(1)}, bf16[440,128]{1,0:T(8,128)(2,1)S(1)}, u32[]{:S(2)}, u32[]{:S(2)}) collective-permute-start(bf16[440,128]{1,0:T(8,128)(2,1)S(1)} %collective-permute-done.11), channel_id=1, source_target_pairs={{0,8},{4,12},{8,16},{12,20},{16,24},{20,28},{24,32},{28,36},{32,40... | collective-permute-start | bytes 337928 | tf_op jit(solution)/shard_map/ppermute | solution.py:183
  59.4 11.2 %collective-permute-start.10 = (bf16[440,128]{1,0:T(8,128)(2,1)S(1)}, bf16[440,128]{1,0:T(8,128)(2,1)S(1)}, u32[]{:S(2)}, u32[]{:S(2)}) collective-permute-start(bf16[440,128]{1,0:T(8,128)(2,1)S(1)} %collective-permute-done.9), channel_id=1, source_target_pairs={{8,0},{12,4},{16,8},{20,12},{24,16},{28,20},{32,24},{36,28},{40,32... | collective-permute-start | bytes 337928 | tf_op jit(solution)/shard_map/ppermute | solution.py:183
  62.2 29.1 %collective-permute-start.37 = (bf16[2160,128]{1,0:T(8,128)(2,1)S(1)}, bf16[2160,128]{1,0:T(8,128)(2,1)S(1)}, u32[]{:S(2)}, u32[]{:S(2)}) collective-permute-start(bf16[2160,128]{1,0:T(8,128)(2,1)S(1)} %constant_dynamic-update-slice_fusion.9.refs_0_), channel_id=1, source_target_pairs={{0,4},{4,0},{8,12},{12,8},{16,20},{20,16},{24,28},{28,24},{32,36},... | collective-permute-start | bytes 1658888 | tf_op jit(solution)/shard_map/ppermute | solution.py:183
  67.9 5.7 %collective-permute-start.34 = (bf16[432,128]{1,0:T(8,128)(2,1)S(1)}, bf16[432,128]{1,0:T(8,128)(2,1)S(1)}, u32[]{:S(2)}, u32[]{:S(2)}) collective-permute-start(bf16[432,128]{1,0:T(8,128)(2,1)S(1)} %collective-permute-done.32), channel_id=1, source_target_pairs={{0,8},{4,12},{8,16},{12,20},{16,24},{20,28},{24,32},{28,36},{32,40... | collective-permute-start | bytes 331784 | tf_op jit(solution)/shard_map/ppermute | solution.py:183
  68.0 6.8 %collective-permute-start.33 = (bf16[432,128]{1,0:T(8,128)(2,1)S(1)}, bf16[432,128]{1,0:T(8,128)(2,1)S(1)}, u32[]{:S(2)}, u32[]{:S(2)}) collective-permute-start(bf16[432,128]{1,0:T(8,128)(2,1)S(1)} %collective-permute-done.30), channel_id=1, source_target_pairs={{8,0},{12,4},{16,8},{20,12},{24,16},{28,20},{32,24},{36,28},{40,32... | collective-permute-start | bytes 331784 | tf_op jit(solution)/shard_map/ppermute | solution.py:183
  70.7 23.0 %collective-permute-start.17 = (bf16[2200,128]{1,0:T(8,128)(2,1)S(1)}, bf16[2200,128]{1,0:T(8,128)(2,1)S(1)}, u32[]{:S(2)}, u32[]{:S(2)}) collective-permute-start(bf16[2200,128]{1,0:T(8,128)(2,1)S(1)} %constant_dynamic-update-slice_fusion.refs_0_), channel_id=1, source_target_pairs={{0,4},{4,0},{8,12},{12,8},{16,20},{20,16},{24,28},{28,24},{32,36},... | collective-permute-start | bytes 1689608 | tf_op jit(solution)/shard_map/ppermute | solution.py:183
  71.7 7.9 %collective-permute-start.14 = (bf16[440,128]{1,0:T(8,128)(2,1)S(1)}, bf16[440,128]{1,0:T(8,128)(2,1)S(1)}, u32[]{:S(2)}, u32[]{:S(2)}) collective-permute-start(bf16[440,128]{1,0:T(8,128)(2,1)S(1)} %collective-permute-done.12), channel_id=1, source_target_pairs={{0,8},{4,12},{8,16},{12,20},{16,24},{20,28},{24,32},{28,36},{32,40... | collective-permute-start | bytes 337928 | tf_op jit(solution)/shard_map/ppermute | solution.py:183
  74.8 7.4 %collective-permute-start.35 = (bf16[224,128]{1,0:T(8,128)(2,1)S(1)}, bf16[224,128]{1,0:T(8,128)(2,1)S(1)}, u32[]{:S(2)}, u32[]{:S(2)}) collective-permute-start(bf16[224,128]{1,0:T(8,128)(2,1)S(1)} %slice.214), channel_id=1, source_target_pairs={{0,8},{4,12},{8,16},{12,20},{16,24},{20,28},{24,32},{28,36},{32,40... | collective-permute-start | bytes 172040 | tf_op jit(solution)/shard_map/ppermute | solution.py:183
  79.6 11.6 %collective-permute-start.38 = (bf16[864,128]{1,0:T(8,128)(2,1)S(1)}, bf16[864,128]{1,0:T(8,128)(2,1)S(1)}, u32[]{:S(2)}, u32[]{:S(2)}) collective-permute-start(bf16[864,128]{1,0:T(8,128)(2,1)S(1)} %constant_dynamic-update-slice_fusion.14.refs_1_), channel_id=1, source_target_pairs={{0,4},{4,0},{8,12},{12,8},{16,20},{20,16},{24,28},{28,24},{32,36},... | collective-permute-start | bytes 663560 | tf_op jit(solution)/shard_map/ppermute | solution.py:183
  86.9 6.8 %collective-permute-start.18 = (bf16[880,128]{1,0:T(8,128)(2,1)S(1)}, bf16[880,128]{1,0:T(8,128)(2,1)S(1)}, u32[]{:S(2)}, u32[]{:S(2)}) collective-permute-start(bf16[880,128]{1,0:T(8,128)(2,1)S(1)} %constant_dynamic-update-slice_fusion.5.refs_1_), channel_id=1, source_target_pairs={{0,4},{4,0},{8,12},{12,8},{16,20},{20,16},{24,28},{28,24},{32,36},... | collective-permute-start | bytes 675848 | tf_op jit(solution)/shard_map/ppermute | solution.py:183
  (22 other events, 156.7 us)

commit v2 on v1

--- a/solution.py
+++ b/solution.py
@@ -1,3 +1,5 @@
+import functools
+
 import jax
 import jax.numpy as jnp
 from jax import lax
@@ -8,8 +10,8 @@
 learn_rate = 0.3
 
 ROWS = (440, 432)
-CUT = 224
-GROUPS = ((0, 1, 2, 6, 7), (3, 5), (4,))
+EARLY, LATE = (4, 5), (0, 1, 2, 3, 6, 7)
+GROUPS = ((0, 7, 1), (6, 2), (5, 3), (4,))
 f32, bf16 = jnp.float32, jnp.bfloat16
 whole = pl.BlockSpec(memory_space=pltpu.VMEM)
 scalars = pl.BlockSpec(memory_space=pltpu.SMEM)
@@ -45,14 +47,22 @@
             yield k, shift, 2 * ((at[0] + k) % 8) + (at[1] + shift) % 2
 
 
-def pack_first_body(at, up, query, key, norm, mine, theirs, q, k_, rows16):
+def pack_first_body(at, up_h, query_h, key_h, norm_h, mine, early, late, up, query, key, norm, q, k_, rows16, sems):
+    pairs = ((query_h, query), (key_h, key), (norm_h, norm), (up_h, up))
+    copies = [pltpu.make_async_copy(x, y, sems.at[i]) for i, (x, y) in enumerate(pairs)]
+    for copy in copies:
+        copy.start()
+    copies[0].wait()
     turn(query, q)
+    copies[1].wait()
     turn(key, k_)
+    copies[2].wait()
     rows16[...] = jnp.zeros((16, 128), f32)
     for r in range(16):
         rows16[r : r + 1, :48] = norm[:, 48 * r : 48 * r + 48]
+    copies[3].wait()
     for k, shift, r in chunks(at):
-        out = (mine, theirs)[shift]
+        out, k = (mine, k) if not shift else (early, k - 4) if k in EARLY else (late, LATE.index(k))
         rows = pl.ds(pl.multiple_of(48 * r, 8), 48)
         for j in range(6):
             out[k, 48 * j : 48 * j + 48, :] = up[0, rows, 128 * j : 128 * j + 128]
@@ -78,10 +88,13 @@
 
 
 def pack_first(at, up, query, key, norm):
+    far = pl.BlockSpec(memory_space=pltpu.HBM)
     return kernel(
-        pack_first_body, [jax.ShapeDtypeStruct((8, 440, 128), f32)] * 2, [scalars] + [whole] * 4,
-        [pltpu.VMEM((768, 256), f32)] * 2 + [pltpu.VMEM((16, 128), f32)],
-    )(at, up, query, key, norm)
+        pack_first_body, [jax.ShapeDtypeStruct((n, 440, 128), f32) for n in (8, 2, 6)], [scalars] + [far] * 4,
+        [pltpu.VMEM(x.shape, f32) for x in (up, query, key, norm)]
+        + [pltpu.VMEM((768, 256), f32)] * 2
+        + [pltpu.VMEM((16, 128), f32), pltpu.SemaphoreType.DMA((4,))],
+    )(at, *(pltpu.with_memory_space_constraint(x, pltpu.HBM) for x in (up, query, key, norm)))
 
 
 def pack_second(at, down, value, mixed):
@@ -113,9 +126,52 @@
     norm[...] = first[432:433, :48]
 
 
+def own_chunk(mine, pair, k):
+    if pair[0].shape[0] == 8:
+        return mine[k] + pair[0][k]
+    return mine[k] + (pair[0][k - 4] if k in EARLY else pair[1][LATE.index(k)])
+
+
+def begin_body(ks, mine, *refs):
+    *pair, a, b = refs
+    a[...] = own_chunk(mine, pair, ks[0])
+    b[...] = own_chunk(mine, pair, ks[1])
+
+
+def add_body(ks, mine, *refs):
+    *pair, got_a, got_b, a, b = refs
+    a[...] = got_a[...] + own_chunk(mine, pair, ks[0])
+    b[...] = got_b[...] + own_chunk(mine, pair, ks[1])
+
+
+def add_one_body(k, mine, *refs):
+    *pair, got, out = refs
+    out[...] = got[...] + own_chunk(mine, pair, k)
+
+
+def update_body(rate, mine, *refs):
+    *pair, got_a, got_b, p, new, half = refs
+    value = p[...] - rate * (got_a[...] + got_b[...] + own_chunk(mine, pair, 0))
+    new[...] = value
+    half[...] = value.astype(bf16)
+
+
+def join_body(*refs):
+    *inputs, out = refs
+    at = 0
+    for ref in inputs:
+        out[at : at + ref.shape[0], :] = ref[...]
+        at += ref.shape[0]
+
+
+def join(arrays):
+    rows = sum(a.shape[0] for a in arrays)
+    return kernel(join_body, [jax.ShapeDtypeStruct((rows, 128), bf16)], [whole] * len(arrays))(*arrays)[0]
+
+
 def pieces(at, refs, rows):
     for shift in (0, 1):
-        for ref, ks in zip(refs[3 * shift : 3 * shift + 3], GROUPS):
+        for ref, ks in zip(refs[4 * shift : 4 * shift + 4], GROUPS):
             for i, k in enumerate(ks):
                 r = 2 * ((at[0] + k) % 8) + (at[1] + shift) % 2
                 yield r, lambda lo, hi, ref=ref, base=i * rows: ref[base + lo : base + hi, :]
@@ -137,7 +193,7 @@
 
 
 def unpack_first_body(at, *refs):
-    up, query, key, norm, q, k_, rows16 = refs[6:]
+    up, query, key, norm, q, k_, rows16 = refs[8:]
     for r, read in pieces(at, refs, 440):
         rows = pl.ds(pl.multiple_of(48 * r, 16), 48)
         for j in range(6):
@@ -151,7 +207,7 @@
 
 
 def unpack_second_body(at, *refs):
-    down, value, mixed, turned, v, m = refs[6:]
+    down, value, mixed, turned, v, m = refs[8:]
     for r, read in pieces(at, refs, 432):
         rows = pl.ds(pl.multiple_of(48 * r, 16), 48)
         for j in range(6):
@@ -182,37 +238,44 @@
     def send(a, pairs):
         return lax.ppermute(a, "replica", pairs)
 
-    packed = pack_first(at, slope_up, back(slope_query), back(slope_key), slope_norm), pack_second(
-        at, slope_down, back(slope_value), slope_mixed
-    )
+    mine0, early, late = pack_first(at, slope_up, back(slope_query), back(slope_key), slope_norm)
+    early = send(early, partner)
+    mine1, theirs1 = pack_second(at, slope_down, back(slope_value), slope_mixed)
+    pair0 = send(late, partner)
+    pair1 = send(theirs1, partner)
+    packed = (mine0, (early, pair0)), (mine1, (pair1,))
     first, second = kernel(
         pack_params_body, [jax.ShapeDtypeStruct((r, 128), f32) for r in ROWS], [whole] * 7
     )(param_up, back(param_down), param_query, param_key, param_value, back(param_mixed), param_norm.reshape(1, 48))
 
     news, gots, others = [], [], []
-    for (mine, theirs), p in zip(packed, (first, second)):
-        pair = send(theirs, partner)
-        start = lax.optimization_barrier(mine[4] + pair[4])
-        rest = lax.optimization_barrier(tuple(mine[k] + pair[k] for k in range(8) if k != 4))
-        own = [*rest[:4], start, *rest[4:]]
+    for s, ((mine, pair), p) in enumerate(zip(packed, (first, second))):
+        rows = ROWS[s]
+        shape = lambda dtype=f32: jax.ShapeDtypeStruct((rows, 128), dtype)
         ab = lambda a, b: (send(a, right), send(b, left))
-        a, b = ab(own[4][:CUT], own[4][CUT:])
-        a = jnp.concatenate([a + own[3][:CUT], own[3][CUT:]])
-        b = jnp.concatenate([own[5][:CUT], b + own[5][CUT:]])
-        for k in (3, 2, 1):
+        known = (mine, *pair)
+        specs = [whole] * len(known)
+        at_right, at_left = (4, 5) if s == 0 else (3, 4)
+        used = 2 if s == 0 else len(known)
+        a, b = kernel(functools.partial(begin_body, (at_right, at_left)), [shape()] * 2, specs[:used])(*known[:used])
+        for step in range(3):
             a, b = ab(a, b)
-            if k > 1:
-                a, b = a + own[k - 1], b + own[9 - k]
-        new = p - rate * (a + b + own[0])
+            ks = at_right - step - 1, at_left + step + 1
+            if step < 2:
+                a, b = kernel(functools.partial(add_body, ks), [shape()] * 2, specs + [whole] * 2)(*known, a, b)
+        one = kernel(functools.partial(add_one_body, ks[s]), [shape()], specs + [whole])(*known, (a, b)[s])[0]
+        one = send(one, (right, left)[s])
+        a, b = (one, b) if s == 0 else (a, one)
+        new, h = kernel(
+            functools.partial(update_body, rate), [shape(), shape(bf16)], specs + [whole] * 3
+        )(*known, a, b, p)
         news.append(new)
-        h = new.astype(bf16)
-        got = {0: h}
         a, b = h, h
-        for k in range(1, 4):
+        groups = []
+        for step in range(3):
             a, b = ab(a, b)
-            got[8 - k], got[k] = a, b
-        got[4] = jnp.concatenate(ab(a[:CUT], b[CUT:]))
-        groups = [jnp.concatenate([got[k] for k in ks]) for ks in GROUPS]
+            groups.append(join([h, a, b] if step == 0 else [a, b]))
+        groups.append(send((a, b)[s], (right, left)[s]))
         gots.append(groups)
         others.append([send(g, partner) for g in groups])
 
@@ -221,11 +284,11 @@
     shape = lambda *x: jax.ShapeDtypeStruct(x, bf16)
     up, query, key, norm = kernel(
         unpack_first_body, [shape(768, 768), shape(192, 768), shape(192, 768), jax.ShapeDtypeStruct((1, 768), f32)],
-        [scalars] + [whole] * 6, [pltpu.VMEM((768, 256), bf16)] * 2 + [pltpu.VMEM((16, 128), f32)],
+        [scalars] + [whole] * 8, [pltpu.VMEM((768, 256), bf16)] * 2 + [pltpu.VMEM((16, 128), f32)],
     )(at, *gots[0], *others[0])
     down, value, mixed = kernel(
         unpack_second_body, [shape(768, 768), shape(192, 768), shape(192, 768)],
-        [scalars] + [whole] * 6, [pltpu.VMEM((768, 768), bf16)] + [pltpu.VMEM((768, 256), bf16)] * 2,
+        [scalars] + [whole] * 8, [pltpu.VMEM((768, 768), bf16)] + [pltpu.VMEM((768, 256), bf16)] * 2,
     )(at, *gots[1], *others[1])
     nup, ndown, nquery, nkey, nvalue, nmixed, nnorm = nexts
     return (

time: 96.7 us -> 102 us (1.055)
  waiting for transfers between devices: 18.6 us -> 30.6 us
  starting transfers between devices: 62 us -> 54.5 us
  Pallas kernels: 8.76 us -> 11.2 us
  other arithmetic: 1.71 us -> 0.67 us
    ppermute x40 -> x39, waiting for transfers between devices: 18.6 us -> 30.6 us  [send(): return lax.ppermute(a, 'replica', pairs)]
    ppermute x40 -> x39, starting transfers between devices: 62 us -> 54.5 us  [send(): return lax.ppermute(a, 'replica', pairs)]
    pallas_call x1 -> x17, Pallas kernels: 1.28 us -> 3.77 us  [the longest x1 2.96 us: pack_first(): kernel(pack_first_body, [jax.ShapeDtypeStruct((n, 440, 128), f32) for n i...]
    unnamed x38 -> x20, local copies, waits for them, and re-layouts: 3.98 us -> 3.83 us
  transfers between devices with their start and end apart: 40 -> 39, of which waited for: 13 -> 15; matrix products, arithmetic and copies ran while one was open for 1% -> 1% of each run, Pallas kernels for 5% -> 7%
where the time goes in v2:
time: 102 us
  starting transfers between devices  54.5 us (53%)
  waiting for transfers between devices  30.6 us (30%)
  Pallas kernels  11.2 us (11%)
  local copies, waits for them, and re-layouts  3.83 us (4%)
    ppermute x39, starting transfers between devices, send(): return lax.ppermute(a, 'replica', pairs)  54.5 us
    ppermute x39, waiting for transfers between devices, send(): return lax.ppermute(a, 'replica', pairs)  30.6 us
    unnamed x20, local copies, waits for them, and re-layouts  3.83 us
    pallas_call x1, Pallas kernels, pack_first(): kernel(pack_first_body, [jax.ShapeDtypeStruct((n, 440, 128), f32) for n i...  2.96 us
    pallas_call x1, Pallas kernels, shards(): kernel(unpack_second_body, [shape(768, 768), shape(192, 768), shape(192,...  2.45 us
    pallas_call x1, Pallas kernels, shards(): kernel(unpack_first_body, [shape(768, 768), shape(192, 768), shape(192, 7...  2.2 us
  transfers between devices with their start and end apart: 39, of which 15 were waited for; matrix products, arithmetic and copies ran while one was open for 1% of the time, Pallas kernels for 7%

profile of v2, /device:TPU:1, one launch (start us, length us, event | category | flops | bytes accessed | tf_op | source)
XLA Modules:
  0.0 101.8 jit_solution(1627088458207959665)
XLA Ops:
  0.7 1.7 %copy-done = f32[1,768,768]{2,1,0:T(8,128)S(1)} copy-done((f32[1,768,768]{2,1,0:T(8,128)S(1)}, f32[1,768,768]{2,1,0:T(8,128)}, u32[]{:S(2)}) %copy-start) | copy-done | bytes 2359320
  4.5 2.0 %shard_map.256 = (f32[8,432,128]{2,1,0:T(8,128)S(1)}, f32[8,432,128]{2,1,0:T(8,128)S(1)}) custom-call(s32[2]{0:T(128)S(1)} %pad_add_fusion.at, f32[1,768,768]{2,1,0:T(8,128)S(1)} %copy-done, f32[1,192,768]{2,1,0:T(8,128)S(1)} %bitcast.14, f32[1,192,768]{2,1,0:T(8,128)S(1)} %copy-done.2), custom_call_target="tpu_custom_call" | custom-call | tf_op jit(solution)/shard_map/pallas_call | solution.py:101
  6.5 3.3 %collective-permute-start.20 = (f32[8,432,128]{2,1,0:T(8,128)S(1)}, f32[8,432,128]{2,1,0:T(8,128)S(1)}, u32[]{:S(2)}, u32[]{:S(2)}) collective-permute-start(f32[8,432,128]{2,1,0:T(8,128)S(1)} %get-tuple-element.64), channel_id=1, source_target_pairs={{0,4},{4,0},{8,12},{12,8},{16,20},{20,16},{24,28},{28,24},{32,36},... | collective-permute-start | bytes 5308424 | tf_op jit(solution)/shard_map/ppermute | solution.py:239
  9.8 3.0 %shard_map.245 = (f32[8,440,128]{2,1,0:T(8,128)S(1)}, f32[2,440,128]{2,1,0:T(8,128)S(1)}, f32[6,440,128]{2,1,0:T(8,128)S(1)}) custom-call(s32[2]{0:T(128)S(1)} %pad_add_fusion.at, f32[1,768,768]{2,1,0:T(8,128)} %up_h.1, f32[1,192,768]{2,1,0:T(8,128)} %bitcast.18, f32[1,192,768]{2,1,0:T(8,128)} %bitcast.19, f32[1,768]{1,0:T(1,128)} %norm_h.1), custom_call_target="tpu_custom_call" | custom-call | tf_op jit(solution)/shard_map/pallas_call | solution.py:92
  13.3 3.2 %collective-permute-done.refs_0_ = f32[2,440,128]{2,1,0:T(8,128)S(1)} collective-permute-done((f32[2,440,128]{2,1,0:T(8,128)S(1)}, f32[2,440,128]{2,1,0:T(8,128)S(1)}, u32[]{:S(2)}, u32[]{:S(2)}) %collective-permute-start) | collective-permute-done | bytes 450592 | tf_op jit(solution)/shard_map/ppermute | solution.py:239
  16.7 3.9 %collective-permute-start.3 = (f32[440,128]{1,0:T(8,128)S(1)}, f32[440,128]{1,0:T(8,128)S(1)}, u32[]{:S(2)}, u32[]{:S(2)}) collective-permute-start(f32[440,128]{1,0:T(8,128)S(1)} %get-tuple-element.55), channel_id=1, source_target_pairs={{8,0},{12,4},{16,8},{20,12},{24,16},{28,20},{32,24},{36,28},{40,32... | collective-permute-start | bytes 675848 | tf_op jit(solution)/shard_map/ppermute | solution.py:239
  20.7 5.7 %collective-permute-done.2.refs_2_ = f32[440,128]{1,0:T(8,128)S(1)} collective-permute-done((f32[440,128]{1,0:T(8,128)S(1)}, f32[440,128]{1,0:T(8,128)S(1)}, u32[]{:S(2)}, u32[]{:S(2)}) %collective-permute-start.2) | collective-permute-done | bytes 225312 | tf_op jit(solution)/shard_map/ppermute | solution.py:239
  26.5 2.7 %collective-permute-start.5 = (f32[440,128]{1,0:T(8,128)S(1)}, f32[440,128]{1,0:T(8,128)S(1)}, u32[]{:S(2)}, u32[]{:S(2)}) collective-permute-start(f32[440,128]{1,0:T(8,128)S(1)} %get-tuple-element.57), channel_id=1, source_target_pairs={{8,0},{12,4},{16,8},{20,12},{24,16},{28,20},{32,24},{36,28},{40,32... | collective-permute-start | bytes 675848 | tf_op jit(solution)/shard_map/ppermute | solution.py:239
  29.3 2.7 %collective-permute-start.22 = (f32[432,128]{1,0:T(8,128)S(1)}, f32[432,128]{1,0:T(8,128)S(1)}, u32[]{:S(2)}, u32[]{:S(2)}) collective-permute-start(f32[432,128]{1,0:T(8,128)S(1)} %get-tuple-element.66), channel_id=1, source_target_pairs={{8,0},{12,4},{16,8},{20,12},{24,16},{28,20},{32,24},{36,28},{40,32... | collective-permute-start | bytes 663560 | tf_op jit(solution)/shard_map/ppermute | solution.py:239
  32.0 2.1 %collective-permute-done.4.refs_2_ = f32[440,128]{1,0:T(8,128)S(1)} collective-permute-done((f32[440,128]{1,0:T(8,128)S(1)}, f32[440,128]{1,0:T(8,128)S(1)}, u32[]{:S(2)}, u32[]{:S(2)}) %collective-permute-start.4) | collective-permute-done | bytes 225312 | tf_op jit(solution)/shard_map/ppermute | solution.py:239
  35.3 3.5 %collective-permute-done.21.refs_1_ = f32[432,128]{1,0:T(8,128)S(1)} collective-permute-done((f32[432,128]{1,0:T(8,128)S(1)}, f32[432,128]{1,0:T(8,128)S(1)}, u32[]{:S(2)}, u32[]{:S(2)}) %collective-permute-start.21) | collective-permute-done | bytes 221216 | tf_op jit(solution)/shard_map/ppermute | solution.py:239
  38.9 1.1 %collective-permute-start.23 = (f32[432,128]{1,0:T(8,128)S(1)}, f32[432,128]{1,0:T(8,128)S(1)}, u32[]{:S(2)}, u32[]{:S(2)}) collective-permute-start(f32[432,128]{1,0:T(8,128)S(1)} %get-tuple-element.67), channel_id=1, source_target_pairs={{0,8},{4,12},{8,16},{12,20},{16,24},{20,28},{24,32},{28,36},{32,40... | collective-permute-start | bytes 663560 | tf_op jit(solution)/shard_map/ppermute | solution.py:239
  40.0 1.6 %collective-permute-start.24 = (f32[432,128]{1,0:T(8,128)S(1)}, f32[432,128]{1,0:T(8,128)S(1)}, u32[]{:S(2)}, u32[]{:S(2)}) collective-permute-start(f32[432,128]{1,0:T(8,128)S(1)} %get-tuple-element.68), channel_id=1, source_target_pairs={{8,0},{12,4},{16,8},{20,12},{24,16},{28,20},{32,24},{36,28},{40,32... | collective-permute-start | bytes 663560 | tf_op jit(solution)/shard_map/ppermute | solution.py:239
  41.6 1.2 %collective-permute-start.8 = (f32[440,128]{1,0:T(8,128)S(1)}, f32[440,128]{1,0:T(8,128)S(1)}, u32[]{:S(2)}, u32[]{:S(2)}) collective-permute-start(f32[440,128]{1,0:T(8,128)S(1)} %get-tuple-element.59), channel_id=1, source_target_pairs={{8,0},{12,4},{16,8},{20,12},{24,16},{28,20},{32,24},{36,28},{40,32... | collective-permute-start | bytes 675848 | tf_op jit(solution)/shard_map/ppermute | solution.py:239
  43.8 4.3 %collective-permute-done.23.refs_1_ = f32[432,128]{1,0:T(8,128)S(1)} collective-permute-done((f32[432,128]{1,0:T(8,128)S(1)}, f32[432,128]{1,0:T(8,128)S(1)}, u32[]{:S(2)}, u32[]{:S(2)}) %collective-permute-start.23) | collective-permute-done | bytes 221216 | tf_op jit(solution)/shard_map/ppermute | solution.py:239
  49.4 3.1 %collective-permute-done.7.refs_2_ = f32[440,128]{1,0:T(8,128)S(1)} collective-permute-done((f32[440,128]{1,0:T(8,128)S(1)}, f32[440,128]{1,0:T(8,128)S(1)}, u32[]{:S(2)}, u32[]{:S(2)}) %collective-permute-start.7) | collective-permute-done | bytes 225312 | tf_op jit(solution)/shard_map/ppermute | solution.py:239
  52.7 2.7 %collective-permute-start.10 = (bf16[440,128]{1,0:T(8,128)(2,1)S(1)}, bf16[440,128]{1,0:T(8,128)(2,1)S(1)}, u32[]{:S(2)}, u32[]{:S(2)}) collective-permute-start(bf16[440,128]{1,0:T(8,128)(2,1)S(1)} %get-tuple-element.61.refs_0_), channel_id=1, source_target_pairs={{8,0},{12,4},{16,8},{20,12},{24,16},{28,20},{32,24},{36,28},{40,32... | collective-permute-start | bytes 337928 | tf_op jit(solution)/shard_map/ppermute | solution.py:239
  55.4 2.2 %collective-permute-done.9.refs_1_ = bf16[440,128]{1,0:T(8,128)(2,1)S(1)} collective-permute-done((bf16[440,128]{1,0:T(8,128)(2,1)S(1)}, bf16[440,128]{1,0:T(8,128)(2,1)S(1)}, u32[]{:S(2)}, u32[]{:S(2)}) %collective-permute-start.9) | collective-permute-done | bytes 112672 | tf_op jit(solution)/shard_map/ppermute | solution.py:239
  57.9 3.0 %collective-permute-start.12 = (bf16[440,128]{1,0:T(8,128)(2,1)S(1)}, bf16[440,128]{1,0:T(8,128)(2,1)S(1)}, u32[]{:S(2)}, u32[]{:S(2)}) collective-permute-start(bf16[440,128]{1,0:T(8,128)(2,1)S(1)} %collective-permute-done.10.refs_2_), channel_id=1, source_target_pairs={{8,0},{12,4},{16,8},{20,12},{24,16},{28,20},{32,24},{36,28},{40,32... | collective-permute-start | bytes 337928 | tf_op jit(solution)/shard_map/ppermute | solution.py:239
  61.0 2.7 %collective-permute-start.27 = (f32[432,128]{1,0:T(8,128)S(1)}, f32[432,128]{1,0:T(8,128)S(1)}, u32[]{:S(2)}, u32[]{:S(2)}) collective-permute-start(f32[432,128]{1,0:T(8,128)S(1)} %shard_map.260), channel_id=1, source_target_pairs={{8,0},{12,4},{16,8},{20,12},{24,16},{28,20},{32,24},{36,28},{40,32... | collective-permute-start | bytes 663560 | tf_op jit(solution)/shard_map/ppermute | solution.py:239
  63.7 4.5 %collective-permute-start.17 = (bf16[880,128]{1,0:T(8,128)(2,1)S(1)}, bf16[880,128]{1,0:T(8,128)(2,1)S(1)}, u32[]{:S(2)}, u32[]{:S(2)}) collective-permute-start(bf16[880,128]{1,0:T(8,128)(2,1)S(1)} %shard_map.253.refs_1_), channel_id=1, source_target_pairs={{0,4},{4,0},{8,12},{12,8},{16,20},{20,16},{24,28},{28,24},{32,36},... | collective-permute-start | bytes 675848 | tf_op jit(solution)/shard_map/ppermute | solution.py:239
  69.5 1.9 %collective-permute-start.14 = (bf16[440,128]{1,0:T(8,128)(2,1)S(1)}, bf16[440,128]{1,0:T(8,128)(2,1)S(1)}, u32[]{:S(2)}, u32[]{:S(2)}) collective-permute-start(bf16[440,128]{1,0:T(8,128)(2,1)S(1)} %collective-permute-done.12.refs_1_), channel_id=1, source_target_pairs={{8,0},{12,4},{16,8},{20,12},{24,16},{28,20},{32,24},{36,28},{40,32... | collective-permute-start | bytes 337928 | tf_op jit(solution)/shard_map/ppermute | solution.py:239
  71.6 3.0 %collective-permute-done.13.refs_0_ = bf16[440,128]{1,0:T(8,128)(2,1)S(1)} collective-permute-done((bf16[440,128]{1,0:T(8,128)(2,1)S(1)}, bf16[440,128]{1,0:T(8,128)(2,1)S(1)}, u32[]{:S(2)}, u32[]{:S(2)}) %collective-permute-start.13) | collective-permute-done | bytes 112672 | tf_op jit(solution)/shard_map/ppermute | solution.py:239
  74.6 1.2 %collective-permute-start.29 = (bf16[432,128]{1,0:T(8,128)(2,1)S(1)}, bf16[432,128]{1,0:T(8,128)(2,1)S(1)}, u32[]{:S(2)}, u32[]{:S(2)}) collective-permute-start(bf16[432,128]{1,0:T(8,128)(2,1)S(1)} %get-tuple-element.72.refs_0_), channel_id=1, source_target_pairs={{8,0},{12,4},{16,8},{20,12},{24,16},{28,20},{32,24},{36,28},{40,32... | collective-permute-start | bytes 331784 | tf_op jit(solution)/shard_map/ppermute | solution.py:239
  76.8 1.6 %collective-permute-start.18 = (bf16[880,128]{1,0:T(8,128)(2,1)S(1)}, bf16[880,128]{1,0:T(8,128)(2,1)S(1)}, u32[]{:S(2)}, u32[]{:S(2)}) collective-permute-start(bf16[880,128]{1,0:T(8,128)(2,1)S(1)} %shard_map.254.refs_2_), channel_id=1, source_target_pairs={{0,4},{4,0},{8,12},{12,8},{16,20},{20,16},{24,28},{28,24},{32,36},... | collective-permute-start | bytes 675848 | tf_op jit(solution)/shard_map/ppermute | solution.py:239
  78.5 2.8 %collective-permute-start.31 = (bf16[432,128]{1,0:T(8,128)(2,1)S(1)}, bf16[432,128]{1,0:T(8,128)(2,1)S(1)}, u32[]{:S(2)}, u32[]{:S(2)}) collective-permute-start(bf16[432,128]{1,0:T(8,128)(2,1)S(1)} %collective-permute-done.29.refs_2_), channel_id=1, source_target_pairs={{8,0},{12,4},{16,8},{20,12},{24,16},{28,20},{32,24},{36,28},{40,32... | collective-permute-start | bytes 331784 | tf_op jit(solution)/shard_map/ppermute | solution.py:239
  83.1 3.1 %collective-permute-start.33 = (bf16[432,128]{1,0:T(8,128)(2,1)S(1)}, bf16[432,128]{1,0:T(8,128)(2,1)S(1)}, u32[]{:S(2)}, u32[]{:S(2)}) collective-permute-start(bf16[432,128]{1,0:T(8,128)(2,1)S(1)} %collective-permute-done.31.refs_1_), channel_id=1, source_target_pairs={{8,0},{12,4},{16,8},{20,12},{24,16},{28,20},{32,24},{36,28},{40,32... | collective-permute-start | bytes 331784 | tf_op jit(solution)/shard_map/ppermute | solution.py:239
  86.2 3.1 %collective-permute-start.35 = (bf16[1296,128]{1,0:T(8,128)(2,1)S(1)}, bf16[1296,128]{1,0:T(8,128)(2,1)S(1)}, u32[]{:S(2)}, u32[]{:S(2)}) collective-permute-start(bf16[1296,128]{1,0:T(8,128)(2,1)S(1)} %shard_map.262.refs_0_), channel_id=1, source_target_pairs={{0,4},{4,0},{8,12},{12,8},{16,20},{20,16},{24,28},{28,24},{32,36},... | collective-permute-start | bytes 995336 | tf_op jit(solution)/shard_map/ppermute | solution.py:239
  89.3 1.1 %collective-permute-start.19 = (bf16[440,128]{1,0:T(8,128)(2,1)S(1)}, bf16[440,128]{1,0:T(8,128)(2,1)S(1)}, u32[]{:S(2)}, u32[]{:S(2)}) collective-permute-start(bf16[440,128]{1,0:T(8,128)(2,1)S(1)} %collective-permute-done.15.refs_3_), channel_id=1, source_target_pairs={{0,4},{4,0},{8,12},{12,8},{16,20},{20,16},{24,28},{28,24},{32,36},... | collective-permute-start | bytes 337928 | tf_op jit(solution)/shard_map/ppermute | solution.py:239
  91.0 4.3 %collective-permute-start.36 = (bf16[864,128]{1,0:T(8,128)(2,1)S(1)}, bf16[864,128]{1,0:T(8,128)(2,1)S(1)}, u32[]{:S(2)}, u32[]{:S(2)}) collective-permute-start(bf16[864,128]{1,0:T(8,128)(2,1)S(1)} %shard_map.263.refs_1_), channel_id=1, source_target_pairs={{0,4},{4,0},{8,12},{12,8},{16,20},{20,16},{24,28},{28,24},{32,36},... | collective-permute-start | bytes 663560 | tf_op jit(solution)/shard_map/ppermute | solution.py:239
  95.4 2.2 %shard_map.255 = (bf16[768,768]{1,0:T(8,128)(2,1)}, bf16[192,768]{1,0:T(8,128)(2,1)}, bf16[192,768]{1,0:T(8,128)(2,1)}, f32[1,768]{1,0:T(1,128)S(1)}) custom-call(s32[2]{0:T(128)S(1)} %pad_add_fusion.at, bf16[1320,128]{1,0:T(8,128)(2,1)S(1)} %shard_map.252.refs_0_, bf16[880,128]{1,0:T(8,128)(2,1)S(1)} %shard_map.253.refs_1_, ...), custom_call_target="tpu_custom_call" | custom-call | tf_op jit(solution)/shard_map/pallas_call | solution.py:285
  99.4 2.4 %shard_map.265 = (bf16[768,768]{1,0:T(8,128)(2,1)}, bf16[192,768]{1,0:T(8,128)(2,1)}, bf16[192,768]{1,0:T(8,128)(2,1)}) custom-call(s32[2]{0:T(128)S(1)} %pad_add_fusion.at, bf16[1296,128]{1,0:T(8,128)(2,1)S(1)} %shard_map.262.refs_0_, bf16[864,128]{1,0:T(8,128)(2,1)S(1)} %shard_map.263.refs_1_, bf16[864,128]{1,0:T(8,128)(2,1)S(1)} %shard_map.264.refs_2_, ...), custom_call_target="tpu_custom_call" | custom-call | tf_op jit(solution)/shard_map/pallas_call | solution.py:289
  (90 shorter events, 14.2 us)
Async XLA Ops:
  6.5 22.7 %collective-permute-start.20 = (f32[8,432,128]{2,1,0:T(8,128)S(1)}, f32[8,432,128]{2,1,0:T(8,128)S(1)}, u32[]{:S(2)}, u32[]{:S(2)}) collective-permute-start(f32[8,432,128]{2,1,0:T(8,128)S(1)} %get-tuple-element.64), channel_id=1, source_target_pairs={{0,4},{4,0},{8,12},{12,8},{16,20},{20,16},{24,28},{28,24},{32,36},... | collective-permute-start | bytes 5308424 | tf_op jit(solution)/shard_map/ppermute | solution.py:239
  12.7 13.6 %collective-permute-start.1 = (f32[6,440,128]{2,1,0:T(8,128)S(1)}, f32[6,440,128]{2,1,0:T(8,128)S(1)}, u32[]{:S(2)}, u32[]{:S(2)}) collective-permute-start(f32[6,440,128]{2,1,0:T(8,128)S(1)} %get-tuple-element.53), channel_id=1, source_target_pairs={{0,4},{4,0},{8,12},{12,8},{16,20},{20,16},{24,28},{28,24},{32,36},... | collective-permute-start | bytes 4055048 | tf_op jit(solution)/shard_map/ppermute | solution.py:239
  16.6 9.7 %collective-permute-start.2 = (f32[440,128]{1,0:T(8,128)S(1)}, f32[440,128]{1,0:T(8,128)S(1)}, u32[]{:S(2)}, u32[]{:S(2)}) collective-permute-start(f32[440,128]{1,0:T(8,128)S(1)} %get-tuple-element.54), channel_id=1, source_target_pairs={{0,8},{4,12},{8,16},{12,20},{16,24},{20,28},{24,32},{28,36},{32,40... | collective-permute-start | bytes 675848 | tf_op jit(solution)/shard_map/ppermute | solution.py:239
  16.7 9.6 %collective-permute-start.3 = (f32[440,128]{1,0:T(8,128)S(1)}, f32[440,128]{1,0:T(8,128)S(1)}, u32[]{:S(2)}, u32[]{:S(2)}) collective-permute-start(f32[440,128]{1,0:T(8,128)S(1)} %get-tuple-element.55), channel_id=1, source_target_pairs={{8,0},{12,4},{16,8},{20,12},{24,16},{28,20},{32,24},{36,28},{40,32... | collective-permute-start | bytes 675848 | tf_op jit(solution)/shard_map/ppermute | solution.py:239
  26.4 7.7 %collective-permute-start.4 = (f32[440,128]{1,0:T(8,128)S(1)}, f32[440,128]{1,0:T(8,128)S(1)}, u32[]{:S(2)}, u32[]{:S(2)}) collective-permute-start(f32[440,128]{1,0:T(8,128)S(1)} %get-tuple-element.56), channel_id=1, source_target_pairs={{0,8},{4,12},{8,16},{12,20},{16,24},{20,28},{24,32},{28,36},{32,40... | collective-permute-start | bytes 675848 | tf_op jit(solution)/shard_map/ppermute | solution.py:239
  26.5 7.6 %collective-permute-start.5 = (f32[440,128]{1,0:T(8,128)S(1)}, f32[440,128]{1,0:T(8,128)S(1)}, u32[]{:S(2)}, u32[]{:S(2)}) collective-permute-start(f32[440,128]{1,0:T(8,128)S(1)} %get-tuple-element.57), channel_id=1, source_target_pairs={{8,0},{12,4},{16,8},{20,12},{24,16},{28,20},{32,24},{36,28},{40,32... | collective-permute-start | bytes 675848 | tf_op jit(solution)/shard_map/ppermute | solution.py:239
  29.2 9.6 %collective-permute-start.21 = (f32[432,128]{1,0:T(8,128)S(1)}, f32[432,128]{1,0:T(8,128)S(1)}, u32[]{:S(2)}, u32[]{:S(2)}) collective-permute-start(f32[432,128]{1,0:T(8,128)S(1)} %get-tuple-element.65), channel_id=1, source_target_pairs={{0,8},{4,12},{8,16},{12,20},{16,24},{20,28},{24,32},{28,36},{32,40... | collective-permute-start | bytes 663560 | tf_op jit(solution)/shard_map/ppermute | solution.py:239
  29.3 9.5 %collective-permute-start.22 = (f32[432,128]{1,0:T(8,128)S(1)}, f32[432,128]{1,0:T(8,128)S(1)}, u32[]{:S(2)}, u32[]{:S(2)}) collective-permute-start(f32[432,128]{1,0:T(8,128)S(1)} %get-tuple-element.66), channel_id=1, source_target_pairs={{8,0},{12,4},{16,8},{20,12},{24,16},{28,20},{32,24},{36,28},{40,32... | collective-permute-start | bytes 663560 | tf_op jit(solution)/shard_map/ppermute | solution.py:239
  34.2 9.2 %collective-permute-start.6 = (f32[440,128]{1,0:T(8,128)S(1)}, f32[440,128]{1,0:T(8,128)S(1)}, u32[]{:S(2)}, u32[]{:S(2)}) collective-permute-start(f32[440,128]{1,0:T(8,128)S(1)} %get-tuple-element.58), channel_id=1, source_target_pairs={{0,8},{4,12},{8,16},{12,20},{16,24},{20,28},{24,32},{28,36},{32,40... | collective-permute-start | bytes 675848 | tf_op jit(solution)/shard_map/ppermute | solution.py:239
  38.9 9.3 %collective-permute-start.23 = (f32[432,128]{1,0:T(8,128)S(1)}, f32[432,128]{1,0:T(8,128)S(1)}, u32[]{:S(2)}, u32[]{:S(2)}) collective-permute-start(f32[432,128]{1,0:T(8,128)S(1)} %get-tuple-element.67), channel_id=1, source_target_pairs={{0,8},{4,12},{8,16},{12,20},{16,24},{20,28},{24,32},{28,36},{32,40... | collective-permute-start | bytes 663560 | tf_op jit(solution)/shard_map/ppermute | solution.py:239
  40.0 8.2 %collective-permute-start.24 = (f32[432,128]{1,0:T(8,128)S(1)}, f32[432,128]{1,0:T(8,128)S(1)}, u32[]{:S(2)}, u32[]{:S(2)}) collective-permute-start(f32[432,128]{1,0:T(8,128)S(1)} %get-tuple-element.68), channel_id=1, source_target_pairs={{8,0},{12,4},{16,8},{20,12},{24,16},{28,20},{32,24},{36,28},{40,32... | collective-permute-start | bytes 663560 | tf_op jit(solution)/shard_map/ppermute | solution.py:239
  41.6 7.8 %collective-permute-start.8 = (f32[440,128]{1,0:T(8,128)S(1)}, f32[440,128]{1,0:T(8,128)S(1)}, u32[]{:S(2)}, u32[]{:S(2)}) collective-permute-start(f32[440,128]{1,0:T(8,128)S(1)} %get-tuple-element.59), channel_id=1, source_target_pairs={{8,0},{12,4},{16,8},{20,12},{24,16},{28,20},{32,24},{36,28},{40,32... | collective-permute-start | bytes 675848 | tf_op jit(solution)/shard_map/ppermute | solution.py:239
  43.6 9.0 %collective-permute-start.7 = (f32[440,128]{1,0:T(8,128)S(1)}, f32[440,128]{1,0:T(8,128)S(1)}, u32[]{:S(2)}, u32[]{:S(2)}) collective-permute-start(f32[440,128]{1,0:T(8,128)S(1)} %shard_map.249), channel_id=1, source_target_pairs={{0,8},{4,12},{8,16},{12,20},{16,24},{20,28},{24,32},{28,36},{32,40... | collective-permute-start | bytes 675848 | tf_op jit(solution)/shard_map/ppermute | solution.py:239
  48.2 12.7 %collective-permute-start.26 = (f32[432,128]{1,0:T(8,128)S(1)}, f32[432,128]{1,0:T(8,128)S(1)}, u32[]{:S(2)}, u32[]{:S(2)}) collective-permute-start(f32[432,128]{1,0:T(8,128)S(1)} %get-tuple-element.70), channel_id=1, source_target_pairs={{8,0},{12,4},{16,8},{20,12},{24,16},{28,20},{32,24},{36,28},{40,32... | collective-permute-start | bytes 663560 | tf_op jit(solution)/shard_map/ppermute | solution.py:239
  52.6 4.9 %collective-permute-start.9 = (bf16[440,128]{1,0:T(8,128)(2,1)S(1)}, bf16[440,128]{1,0:T(8,128)(2,1)S(1)}, u32[]{:S(2)}, u32[]{:S(2)}) collective-permute-start(bf16[440,128]{1,0:T(8,128)(2,1)S(1)} %get-tuple-element.61.refs_0_), channel_id=1, source_target_pairs={{0,8},{4,12},{8,16},{12,20},{16,24},{20,28},{24,32},{28,36},{32,40... | collective-permute-start | bytes 337928 | tf_op jit(solution)/shard_map/ppermute | solution.py:239
  52.7 5.2 %collective-permute-start.10 = (bf16[440,128]{1,0:T(8,128)(2,1)S(1)}, bf16[440,128]{1,0:T(8,128)(2,1)S(1)}, u32[]{:S(2)}, u32[]{:S(2)}) collective-permute-start(bf16[440,128]{1,0:T(8,128)(2,1)S(1)} %get-tuple-element.61.refs_0_), channel_id=1, source_target_pairs={{8,0},{12,4},{16,8},{20,12},{24,16},{28,20},{32,24},{36,28},{40,32... | collective-permute-start | bytes 337928 | tf_op jit(solution)/shard_map/ppermute | solution.py:239
  57.6 6.2 %collective-permute-start.11 = (bf16[440,128]{1,0:T(8,128)(2,1)S(1)}, bf16[440,128]{1,0:T(8,128)(2,1)S(1)}, u32[]{:S(2)}, u32[]{:S(2)}) collective-permute-start(bf16[440,128]{1,0:T(8,128)(2,1)S(1)} %collective-permute-done.9.refs_1_), channel_id=1, source_target_pairs={{0,8},{4,12},{8,16},{12,20},{16,24},{20,28},{24,32},{28,36},{32,40... | collective-permute-start | bytes 337928 | tf_op jit(solution)/shard_map/ppermute | solution.py:239
  57.9 5.8 %collective-permute-start.12 = (bf16[440,128]{1,0:T(8,128)(2,1)S(1)}, bf16[440,128]{1,0:T(8,128)(2,1)S(1)}, u32[]{:S(2)}, u32[]{:S(2)}) collective-permute-start(bf16[440,128]{1,0:T(8,128)(2,1)S(1)} %collective-permute-done.10.refs_2_), channel_id=1, source_target_pairs={{8,0},{12,4},{16,8},{20,12},{24,16},{28,20},{32,24},{36,28},{40,32... | collective-permute-start | bytes 337928 | tf_op jit(solution)/shard_map/ppermute | solution.py:239
  60.9 8.6 %collective-permute-start.25 = (f32[432,128]{1,0:T(8,128)S(1)}, f32[432,128]{1,0:T(8,128)S(1)}, u32[]{:S(2)}, u32[]{:S(2)}) collective-permute-start(f32[432,128]{1,0:T(8,128)S(1)} %get-tuple-element.69), channel_id=1, source_target_pairs={{0,8},{4,12},{8,16},{12,20},{16,24},{20,28},{24,32},{28,36},{32,40... | collective-permute-start | bytes 663560 | tf_op jit(solution)/shard_map/ppermute | solution.py:239
  61.0 10.4 %collective-permute-start.27 = (f32[432,128]{1,0:T(8,128)S(1)}, f32[432,128]{1,0:T(8,128)S(1)}, u32[]{:S(2)}, u32[]{:S(2)}) collective-permute-start(f32[432,128]{1,0:T(8,128)S(1)} %shard_map.260), channel_id=1, source_target_pairs={{8,0},{12,4},{16,8},{20,12},{24,16},{28,20},{32,24},{36,28},{40,32... | collective-permute-start | bytes 663560 | tf_op jit(solution)/shard_map/ppermute | solution.py:239
  63.7 17.6 %collective-permute-start.17 = (bf16[880,128]{1,0:T(8,128)(2,1)S(1)}, bf16[880,128]{1,0:T(8,128)(2,1)S(1)}, u32[]{:S(2)}, u32[]{:S(2)}) collective-permute-start(bf16[880,128]{1,0:T(8,128)(2,1)S(1)} %shard_map.253.refs_1_), channel_id=1, source_target_pairs={{0,4},{4,0},{8,12},{12,8},{16,20},{20,16},{24,28},{28,24},{32,36},... | collective-permute-start | bytes 675848 | tf_op jit(solution)/shard_map/ppermute | solution.py:239
  68.2 6.3 %collective-permute-start.13 = (bf16[440,128]{1,0:T(8,128)(2,1)S(1)}, bf16[440,128]{1,0:T(8,128)(2,1)S(1)}, u32[]{:S(2)}, u32[]{:S(2)}) collective-permute-start(bf16[440,128]{1,0:T(8,128)(2,1)S(1)} %collective-permute-done.11.refs_0_), channel_id=1, source_target_pairs={{0,8},{4,12},{8,16},{12,20},{16,24},{20,28},{24,32},{28,36},{32,40... | collective-permute-start | bytes 337928 | tf_op jit(solution)/shard_map/ppermute | solution.py:239
  69.0 22.0 %collective-permute-start.16 = (bf16[1320,128]{1,0:T(8,128)(2,1)S(1)}, bf16[1320,128]{1,0:T(8,128)(2,1)S(1)}, u32[]{:S(2)}, u32[]{:S(2)}) collective-permute-start(bf16[1320,128]{1,0:T(8,128)(2,1)S(1)} %shard_map.252.refs_0_), channel_id=1, source_target_pairs={{0,4},{4,0},{8,12},{12,8},{16,20},{20,16},{24,28},{28,24},{32,36},... | collective-permute-start | bytes 1013768 | tf_op jit(solution)/shard_map/ppermute | solution.py:239
  69.5 7.2 %collective-permute-start.14 = (bf16[440,128]{1,0:T(8,128)(2,1)S(1)}, bf16[440,128]{1,0:T(8,128)(2,1)S(1)}, u32[]{:S(2)}, u32[]{:S(2)}) collective-permute-start(bf16[440,128]{1,0:T(8,128)(2,1)S(1)} %collective-permute-done.12.refs_1_), channel_id=1, source_target_pairs={{8,0},{12,4},{16,8},{20,12},{24,16},{28,20},{32,24},{36,28},{40,32... | collective-permute-start | bytes 337928 | tf_op jit(solution)/shard_map/ppermute | solution.py:239
  71.5 5.2 %collective-permute-start.28 = (bf16[432,128]{1,0:T(8,128)(2,1)S(1)}, bf16[432,128]{1,0:T(8,128)(2,1)S(1)}, u32[]{:S(2)}, u32[]{:S(2)}) collective-permute-start(bf16[432,128]{1,0:T(8,128)(2,1)S(1)} %get-tuple-element.72.refs_0_), channel_id=1, source_target_pairs={{0,8},{4,12},{8,16},{12,20},{16,24},{20,28},{24,32},{28,36},{32,40... | collective-permute-start | bytes 331784 | tf_op jit(solution)/shard_map/ppermute | solution.py:239
  76.8 18.5 %collective-permute-start.18 = (bf16[880,128]{1,0:T(8,128)(2,1)S(1)}, bf16[880,128]{1,0:T(8,128)(2,1)S(1)}, u32[]{:S(2)}, u32[]{:S(2)}) collective-permute-start(bf16[880,128]{1,0:T(8,128)(2,1)S(1)} %shard_map.254.refs_2_), channel_id=1, source_target_pairs={{0,4},{4,0},{8,12},{12,8},{16,20},{20,16},{24,28},{28,24},{32,36},... | collective-permute-start | bytes 675848 | tf_op jit(solution)/shard_map/ppermute | solution.py:239
  81.5 7.8 %collective-permute-start.32 = (bf16[432,128]{1,0:T(8,128)(2,1)S(1)}, bf16[432,128]{1,0:T(8,128)(2,1)S(1)}, u32[]{:S(2)}, u32[]{:S(2)}) collective-permute-start(bf16[432,128]{1,0:T(8,128)(2,1)S(1)} %collective-permute-done.30.refs_0_), channel_id=1, source_target_pairs={{0,8},{4,12},{8,16},{12,20},{16,24},{20,28},{24,32},{28,36},{32,40... | collective-permute-start | bytes 331784 | tf_op jit(solution)/shard_map/ppermute | solution.py:239
  83.1 7.3 %collective-permute-start.33 = (bf16[432,128]{1,0:T(8,128)(2,1)S(1)}, bf16[432,128]{1,0:T(8,128)(2,1)S(1)}, u32[]{:S(2)}, u32[]{:S(2)}) collective-permute-start(bf16[432,128]{1,0:T(8,128)(2,1)S(1)} %collective-permute-done.31.refs_1_), channel_id=1, source_target_pairs={{8,0},{12,4},{16,8},{20,12},{24,16},{28,20},{32,24},{36,28},{40,32... | collective-permute-start | bytes 331784 | tf_op jit(solution)/shard_map/ppermute | solution.py:239
  86.2 13.2 %collective-permute-start.35 = (bf16[1296,128]{1,0:T(8,128)(2,1)S(1)}, bf16[1296,128]{1,0:T(8,128)(2,1)S(1)}, u32[]{:S(2)}, u32[]{:S(2)}) collective-permute-start(bf16[1296,128]{1,0:T(8,128)(2,1)S(1)} %shard_map.262.refs_0_), channel_id=1, source_target_pairs={{0,4},{4,0},{8,12},{12,8},{16,20},{20,16},{24,28},{28,24},{32,36},... | collective-permute-start | bytes 995336 | tf_op jit(solution)/shard_map/ppermute | solution.py:239
  89.3 6.1 %collective-permute-start.19 = (bf16[440,128]{1,0:T(8,128)(2,1)S(1)}, bf16[440,128]{1,0:T(8,128)(2,1)S(1)}, u32[]{:S(2)}, u32[]{:S(2)}) collective-permute-start(bf16[440,128]{1,0:T(8,128)(2,1)S(1)} %collective-permute-done.15.refs_3_), channel_id=1, source_target_pairs={{0,4},{4,0},{8,12},{12,8},{16,20},{20,16},{24,28},{28,24},{32,36},... | collective-permute-start | bytes 337928 | tf_op jit(solution)/shard_map/ppermute | solution.py:239
  90.4 7.1 %collective-permute-start.34 = (bf16[432,128]{1,0:T(8,128)(2,1)S(1)}, bf16[432,128]{1,0:T(8,128)(2,1)S(1)}, u32[]{:S(2)}, u32[]{:S(2)}) collective-permute-start(bf16[432,128]{1,0:T(8,128)(2,1)S(1)} %collective-permute-done.33.refs_1_), channel_id=1, source_target_pairs={{8,0},{12,4},{16,8},{20,12},{24,16},{28,20},{32,24},{36,28},{40,32... | collective-permute-start | bytes 331784 | tf_op jit(solution)/shard_map/ppermute | solution.py:239
  91.0 8.4 %collective-permute-start.36 = (bf16[864,128]{1,0:T(8,128)(2,1)S(1)}, bf16[864,128]{1,0:T(8,128)(2,1)S(1)}, u32[]{:S(2)}, u32[]{:S(2)}) collective-permute-start(bf16[864,128]{1,0:T(8,128)(2,1)S(1)} %shard_map.263.refs_1_), channel_id=1, source_target_pairs={{0,4},{4,0},{8,12},{12,8},{16,20},{20,16},{24,28},{28,24},{32,36},... | collective-permute-start | bytes 663560 | tf_op jit(solution)/shard_map/ppermute | solution.py:239
  (17 other events, 70.9 us)

commit v3 on v2

--- a/solution.py
+++ b/solution.py
@@ -14,15 +14,15 @@
 GROUPS = ((0, 7, 1), (6, 2), (5, 3), (4,))
 f32, bf16 = jnp.float32, jnp.bfloat16
 whole = pl.BlockSpec(memory_space=pltpu.VMEM)
-scalars = pl.BlockSpec(memory_space=pltpu.SMEM)
-
-
-def kernel(body, out_shape, in_specs, scratch=()):
+far = pl.BlockSpec(memory_space=pltpu.HBM)
+
+
+def kernel(body, out_shape, in_specs, scratch=(), out_specs=None):
     return pl.pallas_call(
         body,
         out_shape=out_shape,
         in_specs=in_specs,
-        out_specs=[whole] * len(out_shape),
+        out_specs=out_specs or [whole] * len(out_shape),
         scratch_shapes=scratch,
         compiler_params=pltpu.CompilerParams(vmem_limit_bytes=24 << 20),
     )
@@ -41,13 +41,19 @@
         target[lanes, 128:] = rest.T
 
 
+def own_place():
+    me = lax.axis_index("replica")
+    return lax.div(me, 2), lax.rem(me, 2)
+
+
 def chunks(at):
     for k in range(8):
         for shift in (0, 1):
             yield k, shift, 2 * ((at[0] + k) % 8) + (at[1] + shift) % 2
 
 
-def pack_first_body(at, up_h, query_h, key_h, norm_h, mine, early, late, up, query, key, norm, q, k_, rows16, sems):
+def pack_first_body(up_h, query_h, key_h, norm_h, mine, early, late, up, query, key, norm, q, k_, rows16, sems):
+    at = own_place()
     pairs = ((query_h, query), (key_h, key), (norm_h, norm), (up_h, up))
     copies = [pltpu.make_async_copy(x, y, sems.at[i]) for i, (x, y) in enumerate(pairs)]
     for copy in copies:
@@ -71,14 +77,14 @@
         out[k, 432:440, :] = jnp.broadcast_to(rows16[pl.ds(r, 1), :], (8, 128))
 
 
-def pack_second_body(at, down, value, mixed, mine, theirs, turned, v, m):
+def pack_second_body(down, value, mixed, mine, theirs, turned, v, m):
     for i in range(6):
         for j in range(6):
             block = down[0, 128 * i : 128 * i + 128, 128 * j : 128 * j + 128]
             turned[128 * j : 128 * j + 128, 128 * i : 128 * i + 128] = block.T
     turn(value, v)
     turn(mixed, m)
-    for k, shift, r in chunks(at):
+    for k, shift, r in chunks(own_place()):
         out = (mine, theirs)[shift]
         rows = pl.ds(pl.multiple_of(48 * r, 8), 48)
         for j in range(6):
@@ -87,21 +93,20 @@
             out[k, 288 + 48 * j : 336 + 48 * j, :] = block
 
 
-def pack_first(at, up, query, key, norm):
-    far = pl.BlockSpec(memory_space=pltpu.HBM)
+def pack_first(up, query, key, norm):
     return kernel(
-        pack_first_body, [jax.ShapeDtypeStruct((n, 440, 128), f32) for n in (8, 2, 6)], [scalars] + [far] * 4,
+        pack_first_body, [jax.ShapeDtypeStruct((n, 440, 128), f32) for n in (8, 2, 6)], [far] * 4,
         [pltpu.VMEM(x.shape, f32) for x in (up, query, key, norm)]
         + [pltpu.VMEM((768, 256), f32)] * 2
         + [pltpu.VMEM((16, 128), f32), pltpu.SemaphoreType.DMA((4,))],
-    )(at, *(pltpu.with_memory_space_constraint(x, pltpu.HBM) for x in (up, query, key, norm)))
-
-
-def pack_second(at, down, value, mixed):
+    )(*(pltpu.with_memory_space_constraint(x, pltpu.HBM) for x in (up, query, key, norm)))
+
+
+def pack_second(down, value, mixed):
     return kernel(
-        pack_second_body, [jax.ShapeDtypeStruct((8, 432, 128), f32)] * 2, [scalars] + [whole] * 3,
+        pack_second_body, [jax.ShapeDtypeStruct((8, 432, 128), f32)] * 2, [whole] * 3,
         [pltpu.VMEM((768, 768), f32)] + [pltpu.VMEM((768, 256), f32)] * 2,
-    )(at, down, value, mixed)
+    )(down, value, mixed)
 
 
 def pack_params_body(up, down, query, key, value, mixed, norm, first, second):
@@ -169,9 +174,9 @@
     return kernel(join_body, [jax.ShapeDtypeStruct((rows, 128), bf16)], [whole] * len(arrays))(*arrays)[0]
 
 
-def pieces(at, refs, rows):
-    for shift in (0, 1):
-        for ref, ks in zip(refs[4 * shift : 4 * shift + 4], GROUPS):
+def pieces(at, own, other, groups, rows):
+    for shift, refs in ((0, own), (1, other)):
+        for ref, ks in zip(refs, groups):
             for i, k in enumerate(ks):
                 r = 2 * ((at[0] + k) % 8) + (at[1] + shift) % 2
                 yield r, lambda lo, hi, ref=ref, base=i * rows: ref[base + lo : base + hi, :]
@@ -192,33 +197,64 @@
         target[128:, lanes] = source[lanes, 128:].T[:64]
 
 
-def unpack_first_body(at, *refs):
-    up, query, key, norm, q, k_, rows16 = refs[8:]
-    for r, read in pieces(at, refs, 440):
+def put_first(at, own, other, groups, up, q, k_, rows16):
+    for r, read in pieces(at, own, other, groups, 440):
         rows = pl.ds(pl.multiple_of(48 * r, 16), 48)
         for j in range(6):
             up[rows, 128 * j : 128 * j + 128] = read(48 * j, 48 * j + 48)
         put_pair(rows, read, q, k_)
         rows16[pl.ds(r, 1), :] = read(432, 440)[:1].astype(f32)
+
+
+def open_first_body(*refs):
+    put_first(own_place(), refs[:3], refs[3:6], GROUPS[:3], *refs[6:])
+
+
+def unpack_first_body(
+    own, other, up_in, q_in, k_in, rows_in, up_h, query_h, key_h, norm, up, query, key, q, k_, rows16, sems
+):
+    copies = [
+        pltpu.make_async_copy(x, y, sems.at[i]) for i, (x, y) in enumerate(((up, up_h), (query, query_h), (key, key_h)))
+    ]
+    up[...] = up_in[...]
+    q[...] = q_in[...]
+    k_[...] = k_in[...]
+    rows16[...] = rows_in[...]
+    put_first(own_place(), (own,), (other,), GROUPS[3:], up, q, k_, rows16)
+    copies[0].start()
     turn_back(q, query)
+    copies[1].start()
     turn_back(k_, key)
+    copies[2].start()
     for r in range(16):
         norm[:, 48 * r : 48 * r + 48] = rows16[r : r + 1, :48]
-
-
-def unpack_second_body(at, *refs):
-    down, value, mixed, turned, v, m = refs[8:]
-    for r, read in pieces(at, refs, 432):
+    for copy in copies:
+        copy.wait()
+
+
+def unpack_second_body(*refs):
+    down_h, value_h, mixed_h, down, value, mixed, turned, v, m, sems = refs[8:]
+    for r, read in pieces(own_place(), refs[:4], refs[4:8], GROUPS, 432):
         rows = pl.ds(pl.multiple_of(48 * r, 16), 48)
         for j in range(6):
             turned[rows, 128 * j : 128 * j + 128] = read(48 * j, 48 * j + 48)
         put_pair(rows, read, v, m)
-    for i in range(6):
-        for j in range(6):
+    copies = [
+        pltpu.make_async_copy(down.at[pl.ds(128 * j, 128), :], down_h.at[pl.ds(128 * j, 128), :], sems.at[j])
+        for j in range(6)
+    ]
+    copies += [pltpu.make_async_copy(value, value_h, sems.at[6]), pltpu.make_async_copy(mixed, mixed_h, sems.at[7])]
+    turn_back(v, value)
+    copies[6].start()
+    turn_back(m, mixed)
+    copies[7].start()
+    for j in range(6):
+        for i in range(6):
             block = turned[128 * i : 128 * i + 128, 128 * j : 128 * j + 128]
             down[128 * j : 128 * j + 128, 128 * i : 128 * i + 128] = block.T
-    turn_back(v, value)
-    turn_back(m, mixed)
+        copies[j].start()
+    for copy in copies:
+        copy.wait()
 
 
 def shards(
@@ -227,8 +263,6 @@
 ):
     n = lax.axis_size("replica")
     chips = n // 2
-    me = lax.axis_index("replica")
-    at = jnp.stack([me // 2, me % 2]).astype(jnp.int32)
     partner = [(2 * i + k, 2 * i + 1 - k) for i in range(chips) for k in range(2)]
     right = [(2 * i + k, 2 * ((i + 1) % chips) + k) for i in range(chips) for k in range(2)]
     left = [(d, s) for s, d in right]
@@ -238,9 +272,9 @@
     def send(a, pairs):
         return lax.ppermute(a, "replica", pairs)
 
-    mine0, early, late = pack_first(at, slope_up, back(slope_query), back(slope_key), slope_norm)
+    mine0, early, late = pack_first(slope_up, back(slope_query), back(slope_key), slope_norm)
     early = send(early, partner)
-    mine1, theirs1 = pack_second(at, slope_down, back(slope_value), slope_mixed)
+    mine1, theirs1 = pack_second(slope_down, back(slope_value), slope_mixed)
     pair0 = send(late, partner)
     pair1 = send(theirs1, partner)
     packed = (mine0, (early, pair0)), (mine1, (pair1,))
@@ -282,14 +316,18 @@
     shapes = ((48, 768), (48, 768), (48, 192), (48, 192), (48, 192), (48, 192), (1, 48))
     nexts = kernel(unpack_next_body, [jax.ShapeDtypeStruct(x, f32) for x in shapes], [whole] * 2)(*news)
     shape = lambda *x: jax.ShapeDtypeStruct(x, bf16)
+    wide, row = shape(768, 256), jax.ShapeDtypeStruct((16, 128), f32)
+    opened = kernel(open_first_body, [shape(768, 768), wide, wide, row], [whole] * 6)(*gots[0][:3], *others[0][:3])
     up, query, key, norm = kernel(
         unpack_first_body, [shape(768, 768), shape(192, 768), shape(192, 768), jax.ShapeDtypeStruct((1, 768), f32)],
-        [scalars] + [whole] * 8, [pltpu.VMEM((768, 256), bf16)] * 2 + [pltpu.VMEM((16, 128), f32)],
-    )(at, *gots[0], *others[0])
+        [whole] * 6, [pltpu.VMEM((768, 768), bf16)] + [pltpu.VMEM((192, 768), bf16)] * 2 + [pltpu.VMEM((768, 256), bf16)] * 2
+        + [pltpu.VMEM((16, 128), f32), pltpu.SemaphoreType.DMA((3,))], [far] * 3 + [whole],
+    )(gots[0][3], others[0][3], *opened)
     down, value, mixed = kernel(
         unpack_second_body, [shape(768, 768), shape(192, 768), shape(192, 768)],
-        [scalars] + [whole] * 8, [pltpu.VMEM((768, 768), bf16)] + [pltpu.VMEM((768, 256), bf16)] * 2,
-    )(at, *gots[1], *others[1])
+        [whole] * 8, [pltpu.VMEM((768, 768), bf16)] + [pltpu.VMEM((192, 768), bf16)] * 2 + [pltpu.VMEM((768, 768), bf16)]
+        + [pltpu.VMEM((768, 256), bf16)] * 2 + [pltpu.SemaphoreType.DMA((8,))], [far] * 3,
+    )(*gots[1], *others[1])
     nup, ndown, nquery, nkey, nvalue, nmixed, nnorm = nexts
     return (
         up, down, back(query), back(key), back(value), mixed, norm.reshape(768).astype(bf16),

time: 102 us -> 100 us (0.980)
  Pallas kernels: 11.2 us -> 9.27 us
  transfers between devices with their start and end apart: 39 -> 39, of which waited for: 15 -> 15; matrix products, arithmetic and copies ran while one was open for 1% -> 1% of each run, Pallas kernels for 7% -> 6%
where the time goes in v3:
time: 100 us
  starting transfers between devices  54.5 us (54%)
  waiting for transfers between devices  30.9 us (31%)
  Pallas kernels  9.27 us (9%)
  local copies, waits for them, and re-layouts  3.83 us (4%)
  between operations  1.13 us (1%)
    ppermute x39, starting transfers between devices, send(): return lax.ppermute(a, 'replica', pairs)  54.5 us
    ppermute x39, waiting for transfers between devices, send(): return lax.ppermute(a, 'replica', pairs)  30.9 us
    unnamed x20, local copies, waits for them, and re-layouts  3.83 us
    pallas_call x1, Pallas kernels, pack_first(): kernel(pack_first_body, [jax.ShapeDtypeStruct((n, 440, 128), f32) for n i...  2.42 us
  transfers between devices with their start and end apart: 39, of which 15 were waited for; matrix products, arithmetic and copies ran while one was open for 1% of the time, Pallas kernels for 6%

profile of v3, /device:TPU:1, one launch (start us, length us, event | category | flops | bytes accessed | tf_op | source)
XLA Modules:
  0.0 100.2 jit_solution(1698856690866696129)
XLA Ops:
  0.7 1.7 %copy-done = f32[1,768,768]{2,1,0:T(8,128)S(1)} copy-done((f32[1,768,768]{2,1,0:T(8,128)S(1)}, f32[1,768,768]{2,1,0:T(8,128)}, u32[]{:S(2)}) %copy-start) | copy-done | bytes 2359320
  4.4 1.4 %shard_map.257 = (f32[8,432,128]{2,1,0:T(8,128)S(1)}, f32[8,432,128]{2,1,0:T(8,128)S(1)}) custom-call(f32[1,768,768]{2,1,0:T(8,128)S(1)} %copy-done, f32[1,192,768]{2,1,0:T(8,128)S(1)} %bitcast.12, f32[1,192,768]{2,1,0:T(8,128)S(1)} %copy-done.2), custom_call_target="tpu_custom_call" | custom-call | tf_op jit(solution)/shard_map/pallas_call | solution.py:106
  5.9 3.3 %collective-permute-start.20 = (f32[8,432,128]{2,1,0:T(8,128)S(1)}, f32[8,432,128]{2,1,0:T(8,128)S(1)}, u32[]{:S(2)}, u32[]{:S(2)}) collective-permute-start(f32[8,432,128]{2,1,0:T(8,128)S(1)} %get-tuple-element.72), channel_id=1, source_target_pairs={{0,4},{4,0},{8,12},{12,8},{16,20},{20,16},{24,28},{28,24},{32,36},... | collective-permute-start | bytes 5308424 | tf_op jit(solution)/shard_map/ppermute | solution.py:273
  9.1 2.4 %shard_map.245 = (f32[8,440,128]{2,1,0:T(8,128)S(1)}, f32[2,440,128]{2,1,0:T(8,128)S(1)}, f32[6,440,128]{2,1,0:T(8,128)S(1)}) custom-call(f32[1,768,768]{2,1,0:T(8,128)} %up_h.1, f32[1,192,768]{2,1,0:T(8,128)} %bitcast.16, f32[1,192,768]{2,1,0:T(8,128)} %bitcast.17, f32[1,768]{1,0:T(1,128)} %norm_h.1), custom_call_target="tpu_custom_call" | custom-call | tf_op jit(solution)/shard_map/pallas_call | solution.py:97
  12.2 3.2 %collective-permute-done.refs_0_ = f32[2,440,128]{2,1,0:T(8,128)S(1)} collective-permute-done((f32[2,440,128]{2,1,0:T(8,128)S(1)}, f32[2,440,128]{2,1,0:T(8,128)S(1)}, u32[]{:S(2)}, u32[]{:S(2)}) %collective-permute-start) | collective-permute-done | bytes 450592 | tf_op jit(solution)/shard_map/ppermute | solution.py:273
  15.5 3.9 %collective-permute-start.3 = (f32[440,128]{1,0:T(8,128)S(1)}, f32[440,128]{1,0:T(8,128)S(1)}, u32[]{:S(2)}, u32[]{:S(2)}) collective-permute-start(f32[440,128]{1,0:T(8,128)S(1)} %get-tuple-element.59), channel_id=1, source_target_pairs={{8,0},{12,4},{16,8},{20,12},{24,16},{28,20},{32,24},{36,28},{40,32... | collective-permute-start | bytes 675848 | tf_op jit(solution)/shard_map/ppermute | solution.py:273
  19.5 5.7 %collective-permute-done.2.refs_2_ = f32[440,128]{1,0:T(8,128)S(1)} collective-permute-done((f32[440,128]{1,0:T(8,128)S(1)}, f32[440,128]{1,0:T(8,128)S(1)}, u32[]{:S(2)}, u32[]{:S(2)}) %collective-permute-start.2) | collective-permute-done | bytes 225312 | tf_op jit(solution)/shard_map/ppermute | solution.py:273
  25.3 2.7 %collective-permute-start.5 = (f32[440,128]{1,0:T(8,128)S(1)}, f32[440,128]{1,0:T(8,128)S(1)}, u32[]{:S(2)}, u32[]{:S(2)}) collective-permute-start(f32[440,128]{1,0:T(8,128)S(1)} %get-tuple-element.61), channel_id=1, source_target_pairs={{8,0},{12,4},{16,8},{20,12},{24,16},{28,20},{32,24},{36,28},{40,32... | collective-permute-start | bytes 675848 | tf_op jit(solution)/shard_map/ppermute | solution.py:273
  28.2 2.7 %collective-permute-start.22 = (f32[432,128]{1,0:T(8,128)S(1)}, f32[432,128]{1,0:T(8,128)S(1)}, u32[]{:S(2)}, u32[]{:S(2)}) collective-permute-start(f32[432,128]{1,0:T(8,128)S(1)} %get-tuple-element.74), channel_id=1, source_target_pairs={{8,0},{12,4},{16,8},{20,12},{24,16},{28,20},{32,24},{36,28},{40,32... | collective-permute-start | bytes 663560 | tf_op jit(solution)/shard_map/ppermute | solution.py:273
  30.8 2.1 %collective-permute-done.4.refs_2_ = f32[440,128]{1,0:T(8,128)S(1)} collective-permute-done((f32[440,128]{1,0:T(8,128)S(1)}, f32[440,128]{1,0:T(8,128)S(1)}, u32[]{:S(2)}, u32[]{:S(2)}) %collective-permute-start.4) | collective-permute-done | bytes 225312 | tf_op jit(solution)/shard_map/ppermute | solution.py:273
  34.1 3.5 %collective-permute-done.21.refs_1_ = f32[432,128]{1,0:T(8,128)S(1)} collective-permute-done((f32[432,128]{1,0:T(8,128)S(1)}, f32[432,128]{1,0:T(8,128)S(1)}, u32[]{:S(2)}, u32[]{:S(2)}) %collective-permute-start.21) | collective-permute-done | bytes 221216 | tf_op jit(solution)/shard_map/ppermute | solution.py:273
  37.7 1.1 %collective-permute-start.23 = (f32[432,128]{1,0:T(8,128)S(1)}, f32[432,128]{1,0:T(8,128)S(1)}, u32[]{:S(2)}, u32[]{:S(2)}) collective-permute-start(f32[432,128]{1,0:T(8,128)S(1)} %get-tuple-element.75), channel_id=1, source_target_pairs={{0,8},{4,12},{8,16},{12,20},{16,24},{20,28},{24,32},{28,36},{32,40... | collective-permute-start | bytes 663560 | tf_op jit(solution)/shard_map/ppermute | solution.py:273
  38.9 1.6 %collective-permute-start.24 = (f32[432,128]{1,0:T(8,128)S(1)}, f32[432,128]{1,0:T(8,128)S(1)}, u32[]{:S(2)}, u32[]{:S(2)}) collective-permute-start(f32[432,128]{1,0:T(8,128)S(1)} %get-tuple-element.76), channel_id=1, source_target_pairs={{8,0},{12,4},{16,8},{20,12},{24,16},{28,20},{32,24},{36,28},{40,32... | collective-permute-start | bytes 663560 | tf_op jit(solution)/shard_map/ppermute | solution.py:273
  40.5 1.2 %collective-permute-start.8 = (f32[440,128]{1,0:T(8,128)S(1)}, f32[440,128]{1,0:T(8,128)S(1)}, u32[]{:S(2)}, u32[]{:S(2)}) collective-permute-start(f32[440,128]{1,0:T(8,128)S(1)} %get-tuple-element.63), channel_id=1, source_target_pairs={{8,0},{12,4},{16,8},{20,12},{24,16},{28,20},{32,24},{36,28},{40,32... | collective-permute-start | bytes 675848 | tf_op jit(solution)/shard_map/ppermute | solution.py:273
  42.7 4.3 %collective-permute-done.23.refs_1_ = f32[432,128]{1,0:T(8,128)S(1)} collective-permute-done((f32[432,128]{1,0:T(8,128)S(1)}, f32[432,128]{1,0:T(8,128)S(1)}, u32[]{:S(2)}, u32[]{:S(2)}) %collective-permute-start.23) | collective-permute-done | bytes 221216 | tf_op jit(solution)/shard_map/ppermute | solution.py:273
  48.3 3.2 %collective-permute-done.7.refs_2_ = f32[440,128]{1,0:T(8,128)S(1)} collective-permute-done((f32[440,128]{1,0:T(8,128)S(1)}, f32[440,128]{1,0:T(8,128)S(1)}, u32[]{:S(2)}, u32[]{:S(2)}) %collective-permute-start.7) | collective-permute-done | bytes 225312 | tf_op jit(solution)/shard_map/ppermute | solution.py:273
  51.6 2.7 %collective-permute-start.14 = (bf16[440,128]{1,0:T(8,128)(2,1)S(1)}, bf16[440,128]{1,0:T(8,128)(2,1)S(1)}, u32[]{:S(2)}, u32[]{:S(2)}) collective-permute-start(bf16[440,128]{1,0:T(8,128)(2,1)S(1)} %get-tuple-element.65.refs_0_), channel_id=1, source_target_pairs={{8,0},{12,4},{16,8},{20,12},{24,16},{28,20},{32,24},{36,28},{40,32... | collective-permute-start | bytes 337928 | tf_op jit(solution)/shard_map/ppermute | solution.py:273
  54.3 2.2 %collective-permute-done.9.refs_1_ = bf16[440,128]{1,0:T(8,128)(2,1)S(1)} collective-permute-done((bf16[440,128]{1,0:T(8,128)(2,1)S(1)}, bf16[440,128]{1,0:T(8,128)(2,1)S(1)}, u32[]{:S(2)}, u32[]{:S(2)}) %collective-permute-start.9) | collective-permute-done | bytes 112672 | tf_op jit(solution)/shard_map/ppermute | solution.py:273
  56.8 2.9 %collective-permute-start.15 = (bf16[440,128]{1,0:T(8,128)(2,1)S(1)}, bf16[440,128]{1,0:T(8,128)(2,1)S(1)}, u32[]{:S(2)}, u32[]{:S(2)}) collective-permute-start(bf16[440,128]{1,0:T(8,128)(2,1)S(1)} %collective-permute-done.14.refs_2_), channel_id=1, source_target_pairs={{8,0},{12,4},{16,8},{20,12},{24,16},{28,20},{32,24},{36,28},{40,32... | collective-permute-start | bytes 337928 | tf_op jit(solution)/shard_map/ppermute | solution.py:273
  59.8 2.7 %collective-permute-start.27 = (f32[432,128]{1,0:T(8,128)S(1)}, f32[432,128]{1,0:T(8,128)S(1)}, u32[]{:S(2)}, u32[]{:S(2)}) collective-permute-start(f32[432,128]{1,0:T(8,128)S(1)} %shard_map.261), channel_id=1, source_target_pairs={{8,0},{12,4},{16,8},{20,12},{24,16},{28,20},{32,24},{36,28},{40,32... | collective-permute-start | bytes 663560 | tf_op jit(solution)/shard_map/ppermute | solution.py:273
  62.6 4.5 %collective-permute-start.18 = (bf16[880,128]{1,0:T(8,128)(2,1)S(1)}, bf16[880,128]{1,0:T(8,128)(2,1)S(1)}, u32[]{:S(2)}, u32[]{:S(2)}) collective-permute-start(bf16[880,128]{1,0:T(8,128)(2,1)S(1)} %shard_map.253.refs_1_), channel_id=1, source_target_pairs={{0,4},{4,0},{8,12},{12,8},{16,20},{20,16},{24,28},{28,24},{32,36},... | collective-permute-start | bytes 675848 | tf_op jit(solution)/shard_map/ppermute | solution.py:273
  68.3 1.9 %collective-permute-start.16 = (bf16[440,128]{1,0:T(8,128)(2,1)S(1)}, bf16[440,128]{1,0:T(8,128)(2,1)S(1)}, u32[]{:S(2)}, u32[]{:S(2)}) collective-permute-start(bf16[440,128]{1,0:T(8,128)(2,1)S(1)} %collective-permute-done.15.refs_1_), channel_id=1, source_target_pairs={{8,0},{12,4},{16,8},{20,12},{24,16},{28,20},{32,24},{36,28},{40,32... | collective-permute-start | bytes 337928 | tf_op jit(solution)/shard_map/ppermute | solution.py:273
  70.4 3.0 %collective-permute-done.11.refs_0_ = bf16[440,128]{1,0:T(8,128)(2,1)S(1)} collective-permute-done((bf16[440,128]{1,0:T(8,128)(2,1)S(1)}, bf16[440,128]{1,0:T(8,128)(2,1)S(1)}, u32[]{:S(2)}, u32[]{:S(2)}) %collective-permute-start.11) | collective-permute-done | bytes 112672 | tf_op jit(solution)/shard_map/ppermute | solution.py:273
  73.4 1.2 %collective-permute-start.29 = (bf16[432,128]{1,0:T(8,128)(2,1)S(1)}, bf16[432,128]{1,0:T(8,128)(2,1)S(1)}, u32[]{:S(2)}, u32[]{:S(2)}) collective-permute-start(bf16[432,128]{1,0:T(8,128)(2,1)S(1)} %get-tuple-element.80.refs_0_), channel_id=1, source_target_pairs={{8,0},{12,4},{16,8},{20,12},{24,16},{28,20},{32,24},{36,28},{40,32... | collective-permute-start | bytes 331784 | tf_op jit(solution)/shard_map/ppermute | solution.py:273
  75.6 1.6 %collective-permute-start.19 = (bf16[880,128]{1,0:T(8,128)(2,1)S(1)}, bf16[880,128]{1,0:T(8,128)(2,1)S(1)}, u32[]{:S(2)}, u32[]{:S(2)}) collective-permute-start(bf16[880,128]{1,0:T(8,128)(2,1)S(1)} %shard_map.254.refs_2_), channel_id=1, source_target_pairs={{0,4},{4,0},{8,12},{12,8},{16,20},{20,16},{24,28},{28,24},{32,36},... | collective-permute-start | bytes 675848 | tf_op jit(solution)/shard_map/ppermute | solution.py:273
  77.3 2.8 %collective-permute-start.31 = (bf16[432,128]{1,0:T(8,128)(2,1)S(1)}, bf16[432,128]{1,0:T(8,128)(2,1)S(1)}, u32[]{:S(2)}, u32[]{:S(2)}) collective-permute-start(bf16[432,128]{1,0:T(8,128)(2,1)S(1)} %collective-permute-done.29.refs_2_), channel_id=1, source_target_pairs={{8,0},{12,4},{16,8},{20,12},{24,16},{28,20},{32,24},{36,28},{40,32... | collective-permute-start | bytes 331784 | tf_op jit(solution)/shard_map/ppermute | solution.py:273
  80.7 1.2 %collective-permute-done.31.refs_1_ = bf16[432,128]{1,0:T(8,128)(2,1)S(1)} collective-permute-done((bf16[432,128]{1,0:T(8,128)(2,1)S(1)}, bf16[432,128]{1,0:T(8,128)(2,1)S(1)}, u32[]{:S(2)}, u32[]{:S(2)}) %collective-permute-start.31) | collective-permute-done | bytes 110624 | tf_op jit(solution)/shard_map/ppermute | solution.py:273
  81.9 3.1 %collective-permute-start.33 = (bf16[432,128]{1,0:T(8,128)(2,1)S(1)}, bf16[432,128]{1,0:T(8,128)(2,1)S(1)}, u32[]{:S(2)}, u32[]{:S(2)}) collective-permute-start(bf16[432,128]{1,0:T(8,128)(2,1)S(1)} %collective-permute-done.31.refs_1_), channel_id=1, source_target_pairs={{8,0},{12,4},{16,8},{20,12},{24,16},{28,20},{32,24},{36,28},{40,32... | collective-permute-start | bytes 331784 | tf_op jit(solution)/shard_map/ppermute | solution.py:273
  85.0 3.1 %collective-permute-start.35 = (bf16[1296,128]{1,0:T(8,128)(2,1)S(1)}, bf16[1296,128]{1,0:T(8,128)(2,1)S(1)}, u32[]{:S(2)}, u32[]{:S(2)}) collective-permute-start(bf16[1296,128]{1,0:T(8,128)(2,1)S(1)} %shard_map.263.refs_0_), channel_id=1, source_target_pairs={{0,4},{4,0},{8,12},{12,8},{16,20},{20,16},{24,28},{28,24},{32,36},... | collective-permute-start | bytes 995336 | tf_op jit(solution)/shard_map/ppermute | solution.py:273
  89.8 4.3 %collective-permute-start.36 = (bf16[864,128]{1,0:T(8,128)(2,1)S(1)}, bf16[864,128]{1,0:T(8,128)(2,1)S(1)}, u32[]{:S(2)}, u32[]{:S(2)}) collective-permute-start(bf16[864,128]{1,0:T(8,128)(2,1)S(1)} %shard_map.264.refs_1_), channel_id=1, source_target_pairs={{0,4},{4,0},{8,12},{12,8},{16,20},{20,16},{24,28},{28,24},{32,36},... | collective-permute-start | bytes 663560 | tf_op jit(solution)/shard_map/ppermute | solution.py:273
  94.7 1.6 %shard_map.256 = (bf16[768,768]{1,0:T(8,128)(2,1)}, bf16[192,768]{1,0:T(8,128)(2,1)}, bf16[192,768]{1,0:T(8,128)(2,1)}, f32[1,768]{1,0:T(1,128)S(1)}) custom-call(bf16[440,128]{1,0:T(8,128)(2,1)S(1)} %collective-permute-done.12.own, bf16[440,128]{1,0:T(8,128)(2,1)S(1)} %collective-permute-done.13.other, bf16[768,768]{1,0:T(8,128)(2,1)S(1)} %get-tuple-element.66.up_in, ...), custom_call_target="tpu_custom_call" | custom-call | tf_op jit(solution)/shard_map/pallas_call | solution.py:321
  98.2 1.8 %shard_map.266 = (bf16[768,768]{1,0:T(8,128)(2,1)}, bf16[192,768]{1,0:T(8,128)(2,1)}, bf16[192,768]{1,0:T(8,128)(2,1)}) custom-call(bf16[1296,128]{1,0:T(8,128)(2,1)S(1)} %shard_map.263.refs_0_, bf16[864,128]{1,0:T(8,128)(2,1)S(1)} %shard_map.264.refs_1_, bf16[864,128]{1,0:T(8,128)(2,1)S(1)} %shard_map.265.refs_2_, ...), custom_call_target="tpu_custom_call" | custom-call | tf_op jit(solution)/shard_map/pallas_call | solution.py:326
  (90 shorter events, 14.5 us)
Async XLA Ops:
  5.9 22.1 %collective-permute-start.20 = (f32[8,432,128]{2,1,0:T(8,128)S(1)}, f32[8,432,128]{2,1,0:T(8,128)S(1)}, u32[]{:S(2)}, u32[]{:S(2)}) collective-permute-start(f32[8,432,128]{2,1,0:T(8,128)S(1)} %get-tuple-element.72), channel_id=1, source_target_pairs={{0,4},{4,0},{8,12},{12,8},{16,20},{20,16},{24,28},{28,24},{32,36},... | collective-permute-start | bytes 5308424 | tf_op jit(solution)/shard_map/ppermute | solution.py:273
  11.6 13.6 %collective-permute-start.1 = (f32[6,440,128]{2,1,0:T(8,128)S(1)}, f32[6,440,128]{2,1,0:T(8,128)S(1)}, u32[]{:S(2)}, u32[]{:S(2)}) collective-permute-start(f32[6,440,128]{2,1,0:T(8,128)S(1)} %get-tuple-element.57), channel_id=1, source_target_pairs={{0,4},{4,0},{8,12},{12,8},{16,20},{20,16},{24,28},{28,24},{32,36},... | collective-permute-start | bytes 4055048 | tf_op jit(solution)/shard_map/ppermute | solution.py:273
  15.5 9.7 %collective-permute-start.2 = (f32[440,128]{1,0:T(8,128)S(1)}, f32[440,128]{1,0:T(8,128)S(1)}, u32[]{:S(2)}, u32[]{:S(2)}) collective-permute-start(f32[440,128]{1,0:T(8,128)S(1)} %get-tuple-element.58), channel_id=1, source_target_pairs={{0,8},{4,12},{8,16},{12,20},{16,24},{20,28},{24,32},{28,36},{32,40... | collective-permute-start | bytes 675848 | tf_op jit(solution)/shard_map/ppermute | solution.py:273
  15.5 9.6 %collective-permute-start.3 = (f32[440,128]{1,0:T(8,128)S(1)}, f32[440,128]{1,0:T(8,128)S(1)}, u32[]{:S(2)}, u32[]{:S(2)}) collective-permute-start(f32[440,128]{1,0:T(8,128)S(1)} %get-tuple-element.59), channel_id=1, source_target_pairs={{8,0},{12,4},{16,8},{20,12},{24,16},{28,20},{32,24},{36,28},{40,32... | collective-permute-start | bytes 675848 | tf_op jit(solution)/shard_map/ppermute | solution.py:273
  25.3 7.7 %collective-permute-start.4 = (f32[440,128]{1,0:T(8,128)S(1)}, f32[440,128]{1,0:T(8,128)S(1)}, u32[]{:S(2)}, u32[]{:S(2)}) collective-permute-start(f32[440,128]{1,0:T(8,128)S(1)} %get-tuple-element.60), channel_id=1, source_target_pairs={{0,8},{4,12},{8,16},{12,20},{16,24},{20,28},{24,32},{28,36},{32,40... | collective-permute-start | bytes 675848 | tf_op jit(solution)/shard_map/ppermute | solution.py:273
  25.3 7.6 %collective-permute-start.5 = (f32[440,128]{1,0:T(8,128)S(1)}, f32[440,128]{1,0:T(8,128)S(1)}, u32[]{:S(2)}, u32[]{:S(2)}) collective-permute-start(f32[440,128]{1,0:T(8,128)S(1)} %get-tuple-element.61), channel_id=1, source_target_pairs={{8,0},{12,4},{16,8},{20,12},{24,16},{28,20},{32,24},{36,28},{40,32... | collective-permute-start | bytes 675848 | tf_op jit(solution)/shard_map/ppermute | solution.py:273
  28.1 9.6 %collective-permute-start.21 = (f32[432,128]{1,0:T(8,128)S(1)}, f32[432,128]{1,0:T(8,128)S(1)}, u32[]{:S(2)}, u32[]{:S(2)}) collective-permute-start(f32[432,128]{1,0:T(8,128)S(1)} %get-tuple-element.73), channel_id=1, source_target_pairs={{0,8},{4,12},{8,16},{12,20},{16,24},{20,28},{24,32},{28,36},{32,40... | collective-permute-start | bytes 663560 | tf_op jit(solution)/shard_map/ppermute | solution.py:273
  28.2 9.5 %collective-permute-start.22 = (f32[432,128]{1,0:T(8,128)S(1)}, f32[432,128]{1,0:T(8,128)S(1)}, u32[]{:S(2)}, u32[]{:S(2)}) collective-permute-start(f32[432,128]{1,0:T(8,128)S(1)} %get-tuple-element.74), channel_id=1, source_target_pairs={{8,0},{12,4},{16,8},{20,12},{24,16},{28,20},{32,24},{36,28},{40,32... | collective-permute-start | bytes 663560 | tf_op jit(solution)/shard_map/ppermute | solution.py:273
  33.0 9.3 %collective-permute-start.6 = (f32[440,128]{1,0:T(8,128)S(1)}, f32[440,128]{1,0:T(8,128)S(1)}, u32[]{:S(2)}, u32[]{:S(2)}) collective-permute-start(f32[440,128]{1,0:T(8,128)S(1)} %get-tuple-element.62), channel_id=1, source_target_pairs={{0,8},{4,12},{8,16},{12,20},{16,24},{20,28},{24,32},{28,36},{32,40... | collective-permute-start | bytes 675848 | tf_op jit(solution)/shard_map/ppermute | solution.py:273
  37.7 9.3 %collective-permute-start.23 = (f32[432,128]{1,0:T(8,128)S(1)}, f32[432,128]{1,0:T(8,128)S(1)}, u32[]{:S(2)}, u32[]{:S(2)}) collective-permute-start(f32[432,128]{1,0:T(8,128)S(1)} %get-tuple-element.75), channel_id=1, source_target_pairs={{0,8},{4,12},{8,16},{12,20},{16,24},{20,28},{24,32},{28,36},{32,40... | collective-permute-start | bytes 663560 | tf_op jit(solution)/shard_map/ppermute | solution.py:273
  38.9 8.2 %collective-permute-start.24 = (f32[432,128]{1,0:T(8,128)S(1)}, f32[432,128]{1,0:T(8,128)S(1)}, u32[]{:S(2)}, u32[]{:S(2)}) collective-permute-start(f32[432,128]{1,0:T(8,128)S(1)} %get-tuple-element.76), channel_id=1, source_target_pairs={{8,0},{12,4},{16,8},{20,12},{24,16},{28,20},{32,24},{36,28},{40,32... | collective-permute-start | bytes 663560 | tf_op jit(solution)/shard_map/ppermute | solution.py:273
  40.5 7.8 %collective-permute-start.8 = (f32[440,128]{1,0:T(8,128)S(1)}, f32[440,128]{1,0:T(8,128)S(1)}, u32[]{:S(2)}, u32[]{:S(2)}) collective-permute-start(f32[440,128]{1,0:T(8,128)S(1)} %get-tuple-element.63), channel_id=1, source_target_pairs={{8,0},{12,4},{16,8},{20,12},{24,16},{28,20},{32,24},{36,28},{40,32... | collective-permute-start | bytes 675848 | tf_op jit(solution)/shard_map/ppermute | solution.py:273
  42.4 9.0 %collective-permute-start.7 = (f32[440,128]{1,0:T(8,128)S(1)}, f32[440,128]{1,0:T(8,128)S(1)}, u32[]{:S(2)}, u32[]{:S(2)}) collective-permute-start(f32[440,128]{1,0:T(8,128)S(1)} %shard_map.249), channel_id=1, source_target_pairs={{0,8},{4,12},{8,16},{12,20},{16,24},{20,28},{24,32},{28,36},{32,40... | collective-permute-start | bytes 675848 | tf_op jit(solution)/shard_map/ppermute | solution.py:273
  47.1 12.7 %collective-permute-start.26 = (f32[432,128]{1,0:T(8,128)S(1)}, f32[432,128]{1,0:T(8,128)S(1)}, u32[]{:S(2)}, u32[]{:S(2)}) collective-permute-start(f32[432,128]{1,0:T(8,128)S(1)} %get-tuple-element.78), channel_id=1, source_target_pairs={{8,0},{12,4},{16,8},{20,12},{24,16},{28,20},{32,24},{36,28},{40,32... | collective-permute-start | bytes 663560 | tf_op jit(solution)/shard_map/ppermute | solution.py:273
  51.5 4.9 %collective-permute-start.9 = (bf16[440,128]{1,0:T(8,128)(2,1)S(1)}, bf16[440,128]{1,0:T(8,128)(2,1)S(1)}, u32[]{:S(2)}, u32[]{:S(2)}) collective-permute-start(bf16[440,128]{1,0:T(8,128)(2,1)S(1)} %get-tuple-element.65.refs_0_), channel_id=1, source_target_pairs={{0,8},{4,12},{8,16},{12,20},{16,24},{20,28},{24,32},{28,36},{32,40... | collective-permute-start | bytes 337928 | tf_op jit(solution)/shard_map/ppermute | solution.py:273
  51.6 5.2 %collective-permute-start.14 = (bf16[440,128]{1,0:T(8,128)(2,1)S(1)}, bf16[440,128]{1,0:T(8,128)(2,1)S(1)}, u32[]{:S(2)}, u32[]{:S(2)}) collective-permute-start(bf16[440,128]{1,0:T(8,128)(2,1)S(1)} %get-tuple-element.65.refs_0_), channel_id=1, source_target_pairs={{8,0},{12,4},{16,8},{20,12},{24,16},{28,20},{32,24},{36,28},{40,32... | collective-permute-start | bytes 337928 | tf_op jit(solution)/shard_map/ppermute | solution.py:273
  56.5 6.1 %collective-permute-start.10 = (bf16[440,128]{1,0:T(8,128)(2,1)S(1)}, bf16[440,128]{1,0:T(8,128)(2,1)S(1)}, u32[]{:S(2)}, u32[]{:S(2)}) collective-permute-start(bf16[440,128]{1,0:T(8,128)(2,1)S(1)} %collective-permute-done.9.refs_1_), channel_id=1, source_target_pairs={{0,8},{4,12},{8,16},{12,20},{16,24},{20,28},{24,32},{28,36},{32,40... | collective-permute-start | bytes 337928 | tf_op jit(solution)/shard_map/ppermute | solution.py:273
  56.8 5.7 %collective-permute-start.15 = (bf16[440,128]{1,0:T(8,128)(2,1)S(1)}, bf16[440,128]{1,0:T(8,128)(2,1)S(1)}, u32[]{:S(2)}, u32[]{:S(2)}) collective-permute-start(bf16[440,128]{1,0:T(8,128)(2,1)S(1)} %collective-permute-done.14.refs_2_), channel_id=1, source_target_pairs={{8,0},{12,4},{16,8},{20,12},{24,16},{28,20},{32,24},{36,28},{40,32... | collective-permute-start | bytes 337928 | tf_op jit(solution)/shard_map/ppermute | solution.py:273
  59.8 8.6 %collective-permute-start.25 = (f32[432,128]{1,0:T(8,128)S(1)}, f32[432,128]{1,0:T(8,128)S(1)}, u32[]{:S(2)}, u32[]{:S(2)}) collective-permute-start(f32[432,128]{1,0:T(8,128)S(1)} %get-tuple-element.77), channel_id=1, source_target_pairs={{0,8},{4,12},{8,16},{12,20},{16,24},{20,28},{24,32},{28,36},{32,40... | collective-permute-start | bytes 663560 | tf_op jit(solution)/shard_map/ppermute | solution.py:273
  59.8 10.4 %collective-permute-start.27 = (f32[432,128]{1,0:T(8,128)S(1)}, f32[432,128]{1,0:T(8,128)S(1)}, u32[]{:S(2)}, u32[]{:S(2)}) collective-permute-start(f32[432,128]{1,0:T(8,128)S(1)} %shard_map.261), channel_id=1, source_target_pairs={{8,0},{12,4},{16,8},{20,12},{24,16},{28,20},{32,24},{36,28},{40,32... | collective-permute-start | bytes 663560 | tf_op jit(solution)/shard_map/ppermute | solution.py:273
  62.6 17.6 %collective-permute-start.18 = (bf16[880,128]{1,0:T(8,128)(2,1)S(1)}, bf16[880,128]{1,0:T(8,128)(2,1)S(1)}, u32[]{:S(2)}, u32[]{:S(2)}) collective-permute-start(bf16[880,128]{1,0:T(8,128)(2,1)S(1)} %shard_map.253.refs_1_), channel_id=1, source_target_pairs={{0,4},{4,0},{8,12},{12,8},{16,20},{20,16},{24,28},{28,24},{32,36},... | collective-permute-start | bytes 675848 | tf_op jit(solution)/shard_map/ppermute | solution.py:273
  67.1 6.3 %collective-permute-start.11 = (bf16[440,128]{1,0:T(8,128)(2,1)S(1)}, bf16[440,128]{1,0:T(8,128)(2,1)S(1)}, u32[]{:S(2)}, u32[]{:S(2)}) collective-permute-start(bf16[440,128]{1,0:T(8,128)(2,1)S(1)} %collective-permute-done.10.refs_0_), channel_id=1, source_target_pairs={{0,8},{4,12},{8,16},{12,20},{16,24},{20,28},{24,32},{28,36},{32,40... | collective-permute-start | bytes 337928 | tf_op jit(solution)/shard_map/ppermute | solution.py:273
  67.9 22.0 %collective-permute-start.17 = (bf16[1320,128]{1,0:T(8,128)(2,1)S(1)}, bf16[1320,128]{1,0:T(8,128)(2,1)S(1)}, u32[]{:S(2)}, u32[]{:S(2)}) collective-permute-start(bf16[1320,128]{1,0:T(8,128)(2,1)S(1)} %shard_map.252.refs_0_), channel_id=1, source_target_pairs={{0,4},{4,0},{8,12},{12,8},{16,20},{20,16},{24,28},{28,24},{32,36},... | collective-permute-start | bytes 1013768 | tf_op jit(solution)/shard_map/ppermute | solution.py:273
  68.3 7.2 %collective-permute-start.16 = (bf16[440,128]{1,0:T(8,128)(2,1)S(1)}, bf16[440,128]{1,0:T(8,128)(2,1)S(1)}, u32[]{:S(2)}, u32[]{:S(2)}) collective-permute-start(bf16[440,128]{1,0:T(8,128)(2,1)S(1)} %collective-permute-done.15.refs_1_), channel_id=1, source_target_pairs={{8,0},{12,4},{16,8},{20,12},{24,16},{28,20},{32,24},{36,28},{40,32... | collective-permute-start | bytes 337928 | tf_op jit(solution)/shard_map/ppermute | solution.py:273
  70.3 5.2 %collective-permute-start.28 = (bf16[432,128]{1,0:T(8,128)(2,1)S(1)}, bf16[432,128]{1,0:T(8,128)(2,1)S(1)}, u32[]{:S(2)}, u32[]{:S(2)}) collective-permute-start(bf16[432,128]{1,0:T(8,128)(2,1)S(1)} %get-tuple-element.80.refs_0_), channel_id=1, source_target_pairs={{0,8},{4,12},{8,16},{12,20},{16,24},{20,28},{24,32},{28,36},{32,40... | collective-permute-start | bytes 331784 | tf_op jit(solution)/shard_map/ppermute | solution.py:273
  75.6 18.6 %collective-permute-start.19 = (bf16[880,128]{1,0:T(8,128)(2,1)S(1)}, bf16[880,128]{1,0:T(8,128)(2,1)S(1)}, u32[]{:S(2)}, u32[]{:S(2)}) collective-permute-start(bf16[880,128]{1,0:T(8,128)(2,1)S(1)} %shard_map.254.refs_2_), channel_id=1, source_target_pairs={{0,4},{4,0},{8,12},{12,8},{16,20},{20,16},{24,28},{28,24},{32,36},... | collective-permute-start | bytes 675848 | tf_op jit(solution)/shard_map/ppermute | solution.py:273
  80.4 7.8 %collective-permute-start.32 = (bf16[432,128]{1,0:T(8,128)(2,1)S(1)}, bf16[432,128]{1,0:T(8,128)(2,1)S(1)}, u32[]{:S(2)}, u32[]{:S(2)}) collective-permute-start(bf16[432,128]{1,0:T(8,128)(2,1)S(1)} %collective-permute-done.30.refs_0_), channel_id=1, source_target_pairs={{0,8},{4,12},{8,16},{12,20},{16,24},{20,28},{24,32},{28,36},{32,40... | collective-permute-start | bytes 331784 | tf_op jit(solution)/shard_map/ppermute | solution.py:273
  81.9 7.3 %collective-permute-start.33 = (bf16[432,128]{1,0:T(8,128)(2,1)S(1)}, bf16[432,128]{1,0:T(8,128)(2,1)S(1)}, u32[]{:S(2)}, u32[]{:S(2)}) collective-permute-start(bf16[432,128]{1,0:T(8,128)(2,1)S(1)} %collective-permute-done.31.refs_1_), channel_id=1, source_target_pairs={{8,0},{12,4},{16,8},{20,12},{24,16},{28,20},{32,24},{36,28},{40,32... | collective-permute-start | bytes 331784 | tf_op jit(solution)/shard_map/ppermute | solution.py:273
  85.0 13.2 %collective-permute-start.35 = (bf16[1296,128]{1,0:T(8,128)(2,1)S(1)}, bf16[1296,128]{1,0:T(8,128)(2,1)S(1)}, u32[]{:S(2)}, u32[]{:S(2)}) collective-permute-start(bf16[1296,128]{1,0:T(8,128)(2,1)S(1)} %shard_map.263.refs_0_), channel_id=1, source_target_pairs={{0,4},{4,0},{8,12},{12,8},{16,20},{20,16},{24,28},{28,24},{32,36},... | collective-permute-start | bytes 995336 | tf_op jit(solution)/shard_map/ppermute | solution.py:273
  88.2 6.5 %collective-permute-start.13 = (bf16[440,128]{1,0:T(8,128)(2,1)S(1)}, bf16[440,128]{1,0:T(8,128)(2,1)S(1)}, u32[]{:S(2)}, u32[]{:S(2)}) collective-permute-start(bf16[440,128]{1,0:T(8,128)(2,1)S(1)} %collective-permute-done.12.own), channel_id=1, source_target_pairs={{0,4},{4,0},{8,12},{12,8},{16,20},{20,16},{24,28},{28,24},{32,36},... | collective-permute-start | bytes 337928 | tf_op jit(solution)/shard_map/ppermute | solution.py:273
  89.3 7.1 %collective-permute-start.34 = (bf16[432,128]{1,0:T(8,128)(2,1)S(1)}, bf16[432,128]{1,0:T(8,128)(2,1)S(1)}, u32[]{:S(2)}, u32[]{:S(2)}) collective-permute-start(bf16[432,128]{1,0:T(8,128)(2,1)S(1)} %collective-permute-done.33.refs_1_), channel_id=1, source_target_pairs={{8,0},{12,4},{16,8},{20,12},{24,16},{28,20},{32,24},{36,28},{40,32... | collective-permute-start | bytes 331784 | tf_op jit(solution)/shard_map/ppermute | solution.py:273
  89.8 8.4 %collective-permute-start.36 = (bf16[864,128]{1,0:T(8,128)(2,1)S(1)}, bf16[864,128]{1,0:T(8,128)(2,1)S(1)}, u32[]{:S(2)}, u32[]{:S(2)}) collective-permute-start(bf16[864,128]{1,0:T(8,128)(2,1)S(1)} %shard_map.264.refs_1_), channel_id=1, source_target_pairs={{0,4},{4,0},{8,12},{12,8},{16,20},{20,16},{24,28},{28,24},{32,36},... | collective-permute-start | bytes 663560 | tf_op jit(solution)/shard_map/ppermute | solution.py:273
  (17 other events, 70.9 us)
